TPU v7x, 32 devices: a whole 2x2x4 slice. The times are simulated.
32 devices in a mesh: gx: 4 (over z), gy: 4 (over y, x), gz: 2 (over core).
Axes of the slice: x: 2, y: 2, z: 4, core: 2. Of those that a mesh axis runs over, the one named last changes fastest.
Arguments:
- field: bfloat16 [32, 32, 32, 256], P(None, 'gx', 'gy', 'gz'), may hold values from -6 to 6
- mixing: bfloat16 [32, 32], replicated, may hold values from -1 to 1
- kernel_fine: bfloat16 [3, 3, 3, 32, 32], replicated, may hold values from -0.21875 to 0.21875
- kernel_half: bfloat16 [3, 3, 3, 32, 32], replicated, may hold values from -1.5 to 1.5
- kernel_quarter: bfloat16 [3, 3, 3, 32, 32], replicated, may hold values from -4 to 4
- kernel_eighth: bfloat16 [3, 3, 3, 32, 32], replicated, may hold values from -6 to 6
Outputs:
- layer_out: bfloat16 [32, 32, 32, 256], P(None, 'gx', 'gy', 'gz')
All inputs are finite; a program needn't handle non-finite values.
Results may differ from a plain program's by a relative error of at most 0.008.
Values may be sent and summed in bfloat16 or wider, within the bound.
A program may use at most 128 MiB of HBM per device.

v0:
```python
import jax
import jax.numpy as jnp
from jax import lax
from jax.sharding import PartitionSpec as P


def padded_2(block, sides, width):
    for axis, dim in sides:
        count = lax.axis_size(axis)
        forward = [(i, i + 1) for i in range(count - 1)]
        backward = [(target, source) for source, target in forward]
        low = lax.ppermute(
            lax.slice_in_dim(block, block.shape[dim] - width, None, axis=dim), axis, forward
        )
        high = lax.ppermute(lax.slice_in_dim(block, 0, width, axis=dim), axis, backward)
        block = jnp.concatenate([low, block, high], axis=dim)
    return block


def restrict(values):
    chans, sizex, sizey, sizez = values.shape
    blocks = values.astype(jnp.float32).reshape(chans, sizex // 2, 2, sizey // 2, 2, sizez // 2, 2)
    return jnp.mean(blocks, axis=(2, 4, 6)).astype(jnp.bfloat16)


def conv_valid(padded, kernel):
    result = lax.conv_general_dilated(
        padded[None],
        kernel,
        (1, 1, 1),
        "VALID",
        dimension_numbers=("NCDHW", "DHWIO", "NCDHW"),
        preferred_element_type=jnp.float32,
    )
    return result[0]


def refine_padded(padded, dimension):
    length = padded.shape[dimension]
    inner = lax.slice_in_dim(padded, 1, length - 1, axis=dimension)
    lower = lax.slice_in_dim(padded, 0, length - 2, axis=dimension)
    upper = lax.slice_in_dim(padded, 2, length, axis=dimension)
    even_cells = 0.75 * inner + 0.25 * lower
    odd_cells = 0.75 * inner + 0.25 * upper
    joined = jnp.stack([even_cells, odd_cells], axis=dimension + 1)
    shape_out = list(inner.shape)
    shape_out[dimension] = shape_out[dimension] * 2
    return joined.reshape(shape_out)


def prolong_local(values):
    padded = padded_2(values, (("gx", 1), ("gy", 2), ("gz", 3)), 1)
    current = padded.astype(jnp.float32)
    for dimension in (1, 2, 3):
        current = refine_padded(current, dimension)
    return current


def level_rims(values):
    return padded_2(values, (("gx", 1), ("gy", 2), ("gz", 3)), 1)


def on_device(field, mixing, kernel_fine, kernel_half, kernel_quarter, kernel_eighth):
    kernels = (kernel_fine, kernel_half, kernel_quarter, kernel_eighth)
    outputs = []
    fine_padded = padded_2(field, (("gx", 1), ("gy", 2), ("gz", 3)), 1)
    outputs.append(conv_valid(fine_padded, kernel_fine))
    current = field
    for depth in (1, 2):
        current = restrict(current)
        outputs.append(conv_valid(level_rims(current), kernels[depth]))
    current = restrict(current)
    padded = padded_2(current, (("gx", 1), ("gy", 2), ("gz", 3)), 1)
    outputs.append(conv_valid(padded, kernel_eighth))
    carried = outputs[3].astype(jnp.bfloat16)
    for depth in (2, 1):
        carried = (outputs[depth] + prolong_local(carried)).astype(jnp.bfloat16)
    chans = field.shape[0]
    mixed = jnp.dot(mixing, field.reshape(chans, -1), preferred_element_type=jnp.float32).reshape(
        field.shape
    )
    total = mixed + outputs[0] + prolong_local(carried)
    return jax.nn.gelu(total, approximate=True).astype(jnp.bfloat16)


def solution(mesh):
    placed = (P(None, "gx", "gy", "gz"), P(), P(), P(), P(), P())
    return jax.shard_map(
        on_device, mesh=mesh, in_specs=placed, out_specs=P(None, "gx", "gy", "gz"), check_vma=False
    )
```

profile of v0, /device:TPU:13, one launch (start us, length us, event | category | flops | bytes accessed | tf_op | source)
XLA Modules:
  0.0 209.5 jit_solution(3778737647990511584)
XLA Ops:
  0.0 3.7 %copy.131 = f32[32,8,8,128]{0,3,2,1:T(8,128)} copy(bf16[32,8,8,128]{3,2,1,0:T(8,128)(2,1)} %param.6) | data formatting | bytes 1572864 | tf_op jit(solution)/shard_map/reshape | solution.py:22
  3.7 4.9 %reduce_sum.34 = f32[32,4,4,64]{0,3,2,1:T(8,128)S(1)} reduce(f32[32,4,2,4,2,64,2]{0,6,5,4,3,2,1:T(2,128)} %bitcast.162, f32[]{:T(128)} %constant.8.clone.1), dimensions={2,4,6}, to_apply=%region_0.0 | reduce | flops 229376 | bytes 1179652 | tf_op jit(solution)/shard_map/reduce_sum | solution.py:23
  9.1 3.2 %collective-permute-start.18 = (bf16[32,1,1,16]{0,3,2,1:T(8,128)(2,1)S(1)}, bf16[32,1,1,16]{0,3,2,1:T(8,128)(2,1)S(1)}, u32[]{:S(2)}, u32[]{:S(2)}) collective-permute-start(bf16[32,1,1,16]{0,3,2,1:T(8,128)(2,1)S(1)} %fusion.89), channel_id=1, source_target_pairs={{0,8},{8,16},{16,24},{1,9},{9,17},{17,25},{2,10},{10,18},{18,26},{... | collective-permute-start | bytes 3080 | tf_op jit(solution)/shard_map/ppermute | solution.py:12
  16.7 3.1 %collective-permute-start.20 = (bf16[32,3,1,16]{0,3,2,1:T(8,128)(2,1)S(1)}, bf16[32,3,1,16]{0,3,2,1:T(8,128)(2,1)S(1)}, u32[]{:S(2)}, u32[]{:S(2)}) collective-permute-start(bf16[32,3,1,16]{0,3,2,1:T(8,128)(2,1)S(1)} %pad_maximum_fusion.16), channel_id=1, source_target_pairs={{0,2},{2,4},{4,6},{1,3},{3,5},{5,7},{8,10},{10,12},{12,14},{9,11},... | collective-permute-start | bytes 9224 | tf_op jit(solution)/shard_map/ppermute | solution.py:12
  19.8 3.1 %collective-permute-start.21 = (bf16[32,3,1,16]{0,3,2,1:T(8,128)(2,1)S(1)}, bf16[32,3,1,16]{0,3,2,1:T(8,128)(2,1)S(1)}, u32[]{:S(2)}, u32[]{:S(2)}) collective-permute-start(bf16[32,3,1,16]{0,3,2,1:T(8,128)(2,1)S(1)} %pad_maximum_fusion.16), channel_id=1, source_target_pairs={{2,0},{4,2},{6,4},{3,1},{5,3},{7,5},{10,8},{12,10},{14,12},{11,9},... | collective-permute-start | bytes 9224 | tf_op jit(solution)/shard_map/ppermute | solution.py:15
  25.9 5.1 %collective-permute-start.23 = (bf16[32,3,3,1]{0,3,2,1:T(2,128)(2,1)S(1)}, bf16[32,3,3,1]{0,3,2,1:T(2,128)(2,1)S(1)}, u32[]{:S(2)}, u32[]{:S(2)}) collective-permute-start(bf16[32,3,3,1]{0,3,2,1:T(2,128)(2,1)S(1)} %get-tuple-element.52), channel_id=1, source_target_pairs={{1,0},{3,2},{5,4},{7,6},{9,8},{11,10},{13,12},{15,14},{17,16},{19,... | collective-permute-start | bytes 1736 | tf_op jit(solution)/shard_map/ppermute | solution.py:15
  32.5 3.2 %collective-permute-start.24 = (bf16[32,1,1,16]{0,3,2,1:T(8,128)(2,1)S(1)}, bf16[32,1,1,16]{0,3,2,1:T(8,128)(2,1)S(1)}, u32[]{:S(2)}, u32[]{:S(2)}) collective-permute-start(bf16[32,1,1,16]{0,3,2,1:T(8,128)(2,1)S(1)} %slice_bitcast_fusion.4), channel_id=1, source_target_pairs={{0,8},{8,16},{16,24},{1,9},{9,17},{17,25},{2,10},{10,18},{18,26},{... | collective-permute-start | bytes 3080 | tf_op jit(solution)/shard_map/ppermute | solution.py:12
  37.8 3.2 %collective-permute-start.12 = (bf16[32,1,2,32]{0,3,2,1:T(8,128)(2,1)S(1)}, bf16[32,1,2,32]{0,3,2,1:T(8,128)(2,1)S(1)}, u32[]{:S(2)}, u32[]{:S(2)}) collective-permute-start(bf16[32,1,2,32]{0,3,2,1:T(8,128)(2,1)S(1)} %get-tuple-element.55), channel_id=1, source_target_pairs={{0,8},{8,16},{16,24},{1,9},{9,17},{17,25},{2,10},{10,18},{18,26},{... | collective-permute-start | bytes 12296 | tf_op jit(solution)/shard_map/ppermute | solution.py:12
  45.1 4.3 %collective-permute-start.27 = (bf16[32,3,1,16]{0,3,2,1:T(8,128)(2,1)S(1)}, bf16[32,3,1,16]{0,3,2,1:T(8,128)(2,1)S(1)}, u32[]{:S(2)}, u32[]{:S(2)}) collective-permute-start(bf16[32,3,1,16]{0,3,2,1:T(8,128)(2,1)S(1)} %pad_maximum_fusion.17), channel_id=1, source_target_pairs={{2,0},{4,2},{6,4},{3,1},{5,3},{7,5},{10,8},{12,10},{14,12},{11,9},... | collective-permute-start | bytes 9224 | tf_op jit(solution)/shard_map/ppermute | solution.py:15
  51.5 4.5 %collective-permute-start.29 = (bf16[32,3,3,1]{0,3,2,1:T(2,128)(2,1)S(1)}, bf16[32,3,3,1]{0,3,2,1:T(2,128)(2,1)S(1)}, u32[]{:S(2)}, u32[]{:S(2)}) collective-permute-start(bf16[32,3,3,1]{0,3,2,1:T(2,128)(2,1)S(1)} %get-tuple-element.50), channel_id=1, source_target_pairs={{1,0},{3,2},{5,4},{7,6},{9,8},{11,10},{13,12},{15,14},{17,16},{19,... | collective-permute-start | bytes 1736 | tf_op jit(solution)/shard_map/ppermute | solution.py:15
  57.9 4.8 %collective-permute-start.15 = (bf16[32,4,1,32]{0,3,2,1:T(8,128)(2,1)S(1)}, bf16[32,4,1,32]{0,3,2,1:T(8,128)(2,1)S(1)}, u32[]{:S(2)}, u32[]{:S(2)}) collective-permute-start(bf16[32,4,1,32]{0,3,2,1:T(8,128)(2,1)S(1)} %get-tuple-element.46), channel_id=1, source_target_pairs={{2,0},{4,2},{6,4},{3,1},{5,3},{7,5},{10,8},{12,10},{14,12},{11,9},... | collective-permute-start | bytes 24584 | tf_op jit(solution)/shard_map/ppermute | solution.py:15
  65.1 3.0 %collective-permute-start.17 = (bf16[32,4,4,1]{0,3,2,1:T(2,128)(2,1)S(1)}, bf16[32,4,4,1]{0,3,2,1:T(2,128)(2,1)S(1)}, u32[]{:S(2)}, u32[]{:S(2)}) collective-permute-start(bf16[32,4,4,1]{0,3,2,1:T(2,128)(2,1)S(1)} %get-tuple-element.40), channel_id=1, source_target_pairs={{1,0},{3,2},{5,4},{7,6},{9,8},{11,10},{13,12},{15,14},{17,16},{19,... | collective-permute-start | bytes 3080 | tf_op jit(solution)/shard_map/ppermute | solution.py:15
  70.1 3.2 %collective-permute-start.30 = (bf16[32,1,2,32]{0,2,3,1:T(2,128)(2,1)S(1)}, bf16[32,1,2,32]{0,2,3,1:T(2,128)(2,1)S(1)}, u32[]{:S(2)}, u32[]{:S(2)}) collective-permute-start(bf16[32,1,2,32]{0,2,3,1:T(2,128)(2,1)S(1)} %get-tuple-element.53), channel_id=1, source_target_pairs={{0,8},{8,16},{16,24},{1,9},{9,17},{17,25},{2,10},{10,18},{18,26},{... | collective-permute-start | bytes 12296 | tf_op jit(solution)/shard_map/ppermute | solution.py:12
  75.4 2.4 %collective-permute-done.31 = bf16[32,1,2,32]{0,2,3,1:T(2,128)(2,1)S(1)} collective-permute-done((bf16[32,1,2,32]{0,2,3,1:T(2,128)(2,1)S(1)}, bf16[32,1,2,32]{0,2,3,1:T(2,128)(2,1)S(1)}, u32[]{:S(2)}, u32[]{:S(2)}) %collective-permute-start.31) | collective-permute-done | bytes 4128 | tf_op jit(solution)/shard_map/ppermute | solution.py:15
  79.9 4.8 %collective-permute-start.33 = (bf16[32,4,1,32]{0,2,3,1:T(2,128)(2,1)S(1)}, bf16[32,4,1,32]{0,2,3,1:T(2,128)(2,1)S(1)}, u32[]{:S(2)}, u32[]{:S(2)}) collective-permute-start(bf16[32,4,1,32]{0,2,3,1:T(2,128)(2,1)S(1)} %get-tuple-element.44), channel_id=1, source_target_pairs={{2,0},{4,2},{6,4},{3,1},{5,3},{7,5},{10,8},{12,10},{14,12},{11,9},... | collective-permute-start | bytes 24584 | tf_op jit(solution)/shard_map/ppermute | solution.py:15
  86.7 3.4 %collective-permute-start.7 = (bf16[32,1,4,64]{0,3,2,1:T(8,128)(2,1)S(1)}, bf16[32,1,4,64]{0,3,2,1:T(8,128)(2,1)S(1)}, u32[]{:S(2)}, u32[]{:S(2)}) collective-permute-start(bf16[32,1,4,64]{0,3,2,1:T(8,128)(2,1)S(1)} %get-tuple-element.36), channel_id=1, source_target_pairs={{8,0},{16,8},{24,16},{9,1},{17,9},{25,17},{10,2},{18,10},{26,18},{... | collective-permute-start | bytes 49160 | tf_op jit(solution)/shard_map/ppermute | solution.py:15
  91.4 4.5 %collective-permute-start.35 = (bf16[32,4,4,1]{0,2,3,1:T(4,128)(2,1)S(1)}, bf16[32,4,4,1]{0,2,3,1:T(4,128)(2,1)S(1)}, u32[]{:S(2)}, u32[]{:S(2)}) collective-permute-start(bf16[32,4,4,1]{0,2,3,1:T(4,128)(2,1)S(1)} %get-tuple-element.38), channel_id=1, source_target_pairs={{1,0},{3,2},{5,4},{7,6},{9,8},{11,10},{13,12},{15,14},{17,16},{19,... | collective-permute-start | bytes 3080 | tf_op jit(solution)/shard_map/ppermute | solution.py:15
  97.9 4.3 %collective-permute-start.9 = (bf16[32,6,1,64]{0,3,2,1:T(8,128)(2,1)S(1)}, bf16[32,6,1,64]{0,3,2,1:T(8,128)(2,1)S(1)}, u32[]{:S(2)}, u32[]{:S(2)}) collective-permute-start(bf16[32,6,1,64]{0,3,2,1:T(8,128)(2,1)S(1)} %get-tuple-element.24), channel_id=1, source_target_pairs={{2,0},{4,2},{6,4},{3,1},{5,3},{7,5},{10,8},{12,10},{14,12},{11,9},... | collective-permute-start | bytes 73736 | tf_op jit(solution)/shard_map/ppermute | solution.py:15
  106.2 3.2 %collective-permute-start.11 = (bf16[32,6,6,1]{0,3,2,1:T(2,128)(2,1)S(1)}, bf16[32,6,6,1]{0,3,2,1:T(2,128)(2,1)S(1)}, u32[]{:S(2)}, u32[]{:S(2)}) collective-permute-start(bf16[32,6,6,1]{0,3,2,1:T(2,128)(2,1)S(1)} %get-tuple-element.18), channel_id=1, source_target_pairs={{1,0},{3,2},{5,4},{7,6},{9,8},{11,10},{13,12},{15,14},{17,16},{19,... | collective-permute-start | bytes 6920 | tf_op jit(solution)/shard_map/ppermute | solution.py:15
  115.8 3.4 %collective-permute-start.37 = (bf16[32,1,4,64]{0,2,3,1:T(4,128)(2,1)S(1)}, bf16[32,1,4,64]{0,2,3,1:T(4,128)(2,1)S(1)}, u32[]{:S(2)}, u32[]{:S(2)}) collective-permute-start(bf16[32,1,4,64]{0,2,3,1:T(4,128)(2,1)S(1)} %get-tuple-element.30), channel_id=1, source_target_pairs={{8,0},{16,8},{24,16},{9,1},{17,9},{25,17},{10,2},{18,10},{26,18},{... | collective-permute-start | bytes 49160 | tf_op jit(solution)/shard_map/ppermute | solution.py:15
  121.2 3.4 %collective-permute-start.1 = (bf16[32,1,8,128]{3,0,2,1:T(8,128)(2,1)S(1)}, bf16[32,1,8,128]{3,0,2,1:T(8,128)(2,1)S(1)}, u32[]{:S(2)}, u32[]{:S(2)}) collective-permute-start(bf16[32,1,8,128]{3,0,2,1:T(8,128)(2,1)S(1)} %copy.187), channel_id=1, source_target_pairs={{8,0},{16,8},{24,16},{9,1},{17,9},{25,17},{10,2},{18,10},{26,18},{... | collective-permute-start | bytes 196616 | tf_op jit(solution)/shard_map/ppermute | solution.py:15
  128.7 5.0 %collective-permute-start.39 = (bf16[32,6,1,64]{0,2,3,1:T(2,128)(2,1)S(1)}, bf16[32,6,1,64]{0,2,3,1:T(2,128)(2,1)S(1)}, u32[]{:S(2)}, u32[]{:S(2)}) collective-permute-start(bf16[32,6,1,64]{0,2,3,1:T(2,128)(2,1)S(1)} %get-tuple-element.22), channel_id=1, source_target_pairs={{2,0},{4,2},{6,4},{3,1},{5,3},{7,5},{10,8},{12,10},{14,12},{11,9},... | collective-permute-start | bytes 73736 | tf_op jit(solution)/shard_map/ppermute | solution.py:15
  138.4 4.0 %collective-permute-start.41 = (bf16[32,6,6,1]{3,0,2,1:T(8,128)(2,1)S(1)}, bf16[32,6,6,1]{3,0,2,1:T(8,128)(2,1)S(1)}, u32[]{:S(2)}, u32[]{:S(2)}) collective-permute-start(bf16[32,6,6,1]{3,0,2,1:T(8,128)(2,1)S(1)} %get-tuple-element.26), channel_id=1, source_target_pairs={{1,0},{3,2},{5,4},{7,6},{9,8},{11,10},{13,12},{15,14},{17,16},{19,... | collective-permute-start | bytes 6920 | tf_op jit(solution)/shard_map/ppermute | solution.py:15
  144.3 5.0 %collective-permute-start.3 = (bf16[32,10,1,128]{3,0,2,1:T(8,128)(2,1)S(1)}, bf16[32,10,1,128]{3,0,2,1:T(8,128)(2,1)S(1)}, u32[]{:S(2)}, u32[]{:S(2)}) collective-permute-start(bf16[32,10,1,128]{3,0,2,1:T(8,128)(2,1)S(1)} %get-tuple-element.14), channel_id=1, source_target_pairs={{2,0},{4,2},{6,4},{3,1},{5,3},{7,5},{10,8},{12,10},{14,12},{11,9},... | collective-permute-start | bytes 245768 | tf_op jit(solution)/shard_map/ppermute | solution.py:15
  157.5 4.2 %collective-permute-start.5 = (bf16[32,10,10,1]{0,2,3,1:T(8,128)(2,1)}, bf16[32,10,10,1]{0,2,3,1:T(8,128)(2,1)}, u32[]{:S(2)}, u32[]{:S(2)}) collective-permute-start(bf16[32,10,10,1]{0,2,3,1:T(8,128)(2,1)} %copy.124), channel_id=1, source_target_pairs={{1,0},{3,2},{5,4},{7,6},{9,8},{11,10},{13,12},{15,14},{17,16},{19,... | collective-permute-start | bytes 19208 | tf_op jit(solution)/shard_map/ppermute | solution.py:15
  163.3 3.1 %copy.167 = f32[32,8,8,64,2]{0,2,4,3,1:T(8,128)} copy(f32[32,8,8,64,2]{3,1,2,0,4:T(8,128)S(1)} %pad_maximum_fusion) | data formatting | bytes 2097152 | tf_op jit(solution)/shard_map/stack | solution.py:45
  166.4 3.7 %copy.168 = f32[32,8,8,128]{3,0,2,1:T(8,128)} copy(f32[32,8,8,128]{0,2,3,1:T(8,128)} %bitcast.161) | data formatting | bytes 2097152 | tf_op jit(solution)/shard_map/reshape | solution.py:48
  174.4 6.0 %reshape.91 = bf16[32,10,10,1,8,17]{5,4,0,2,1,3:T(8,128)(2,1)} reshape(bf16[32,10,10,1,136]{4,0,2,1,3:T(8,128)(2,1)S(1)} %pad) | data formatting | bytes 1740800 | tf_op jit(solution)/shard_map/conv_general_dilated | solution.py:27
  180.5 10.2 %copy.128 = bf16[32,10,10,1,8,17]{0,4,5,2,1,3:T(8,128)(2,1)} copy(bf16[32,10,10,1,8,17]{5,4,0,2,1,3:T(8,128)(2,1)} %reshape.91) | data formatting | bytes 1740800 | tf_op jit(solution)/shard_map/conv_general_dilated | solution.py:27
  191.8 9.9 %broadcast_select_fusion = f32[8,8,8,17,32]{4,2,3,1,0:T(8,128)S(1)} fusion(pred[8,17]{0,1:T(8,128)(4,1)S(1)} %copy-done.10, bf16[3,3,3,32,32]{4,3,2,1,0:T(8,128)(2,1)S(1)} %copy-done, bf16[32,10,10,1,7,2]{0,4,5,2,1,3:T(8,128)(2,1)S(1)} %slice.258, bf16[32,10,10,1,8,17]{0,4,5,2,1,3:T(8,128)(2,1)} %copy.128), kind=kOutput, calls=%fused_computation.8 | convolution fusion | flops 484493312 | bytes 2129544 | tf_op jit(solution)/shard_map/conv_general_dilated | solution.py:27
  202.5 2.3 %slice.259 = f32[8,8,1,128,32]{4,1,3,0,2:T(8,128)} slice(f32[8,8,1,136,32]{4,1,3,0,2:T(8,128)S(1)} %bitcast.160), slice={[0:8], [0:8], [0:1], [0:128], [0:32]} | slice | bytes 2097152 | tf_op jit(solution)/shard_map/conv_general_dilated | solution.py:27
  204.8 2.9 %copy.173 = f32[8,8,1,128,32]{3,4,1,0,2:T(8,128)S(1)} copy(f32[8,8,1,128,32]{4,1,3,0,2:T(8,128)} %slice.259) | data formatting | bytes 2097152
  (194 shorter events, 73.3 us)
Async XLA Ops:
  16.7 6.2 %collective-permute-start.20 = (bf16[32,3,1,16]{0,3,2,1:T(8,128)(2,1)S(1)}, bf16[32,3,1,16]{0,3,2,1:T(8,128)(2,1)S(1)}, u32[]{:S(2)}, u32[]{:S(2)}) collective-permute-start(bf16[32,3,1,16]{0,3,2,1:T(8,128)(2,1)S(1)} %pad_maximum_fusion.16), channel_id=1, source_target_pairs={{0,2},{2,4},{4,6},{1,3},{3,5},{5,7},{8,10},{10,12},{12,14},{9,11},... | collective-permute-start | bytes 9224 | tf_op jit(solution)/shard_map/ppermute | solution.py:12
  24.6 6.5 %collective-permute-start.22 = (bf16[32,3,3,1]{0,3,2,1:T(2,128)(2,1)S(1)}, bf16[32,3,3,1]{0,3,2,1:T(2,128)(2,1)S(1)}, u32[]{:S(2)}, u32[]{:S(2)}) collective-permute-start(bf16[32,3,3,1]{0,3,2,1:T(2,128)(2,1)S(1)} %get-tuple-element.51), channel_id=1, source_target_pairs={{0,1},{2,3},{4,5},{6,7},{8,9},{10,11},{12,13},{14,15},{16,17},{18,... | collective-permute-start | bytes 1736 | tf_op jit(solution)/shard_map/ppermute | solution.py:12
  25.9 6.0 %collective-permute-start.23 = (bf16[32,3,3,1]{0,3,2,1:T(2,128)(2,1)S(1)}, bf16[32,3,3,1]{0,3,2,1:T(2,128)(2,1)S(1)}, u32[]{:S(2)}, u32[]{:S(2)}) collective-permute-start(bf16[32,3,3,1]{0,3,2,1:T(2,128)(2,1)S(1)} %get-tuple-element.52), channel_id=1, source_target_pairs={{1,0},{3,2},{5,4},{7,6},{9,8},{11,10},{13,12},{15,14},{17,16},{19,... | collective-permute-start | bytes 1736 | tf_op jit(solution)/shard_map/ppermute | solution.py:15
  32.5 10.6 %collective-permute-start.24 = (bf16[32,1,1,16]{0,3,2,1:T(8,128)(2,1)S(1)}, bf16[32,1,1,16]{0,3,2,1:T(8,128)(2,1)S(1)}, u32[]{:S(2)}, u32[]{:S(2)}) collective-permute-start(bf16[32,1,1,16]{0,3,2,1:T(8,128)(2,1)S(1)} %slice_bitcast_fusion.4), channel_id=1, source_target_pairs={{0,8},{8,16},{16,24},{1,9},{9,17},{17,25},{2,10},{10,18},{18,26},{... | collective-permute-start | bytes 3080 | tf_op jit(solution)/shard_map/ppermute | solution.py:12
  35.7 7.4 %collective-permute-start.25 = (bf16[32,1,1,16]{0,3,2,1:T(8,128)(2,1)S(1)}, bf16[32,1,1,16]{0,3,2,1:T(8,128)(2,1)S(1)}, u32[]{:S(2)}, u32[]{:S(2)}) collective-permute-start(bf16[32,1,1,16]{0,3,2,1:T(8,128)(2,1)S(1)} %slice_bitcast_fusion.4), channel_id=1, source_target_pairs={{8,0},{16,8},{24,16},{9,1},{17,9},{25,17},{10,2},{18,10},{26,18},{... | collective-permute-start | bytes 3080 | tf_op jit(solution)/shard_map/ppermute | solution.py:15
  37.8 11.5 %collective-permute-start.12 = (bf16[32,1,2,32]{0,3,2,1:T(8,128)(2,1)S(1)}, bf16[32,1,2,32]{0,3,2,1:T(8,128)(2,1)S(1)}, u32[]{:S(2)}, u32[]{:S(2)}) collective-permute-start(bf16[32,1,2,32]{0,3,2,1:T(8,128)(2,1)S(1)} %get-tuple-element.55), channel_id=1, source_target_pairs={{0,8},{8,16},{16,24},{1,9},{9,17},{17,25},{2,10},{10,18},{18,26},{... | collective-permute-start | bytes 12296 | tf_op jit(solution)/shard_map/ppermute | solution.py:12
  41.0 8.3 %collective-permute-start.13 = (bf16[32,1,2,32]{0,3,2,1:T(8,128)(2,1)S(1)}, bf16[32,1,2,32]{0,3,2,1:T(8,128)(2,1)S(1)}, u32[]{:S(2)}, u32[]{:S(2)}) collective-permute-start(bf16[32,1,2,32]{0,3,2,1:T(8,128)(2,1)S(1)} %get-tuple-element.56), channel_id=1, source_target_pairs={{8,0},{16,8},{24,16},{9,1},{17,9},{25,17},{10,2},{18,10},{26,18},{... | collective-permute-start | bytes 12296 | tf_op jit(solution)/shard_map/ppermute | solution.py:15
  43.1 6.2 %collective-permute-start.26 = (bf16[32,3,1,16]{0,3,2,1:T(8,128)(2,1)S(1)}, bf16[32,3,1,16]{0,3,2,1:T(8,128)(2,1)S(1)}, u32[]{:S(2)}, u32[]{:S(2)}) collective-permute-start(bf16[32,3,1,16]{0,3,2,1:T(8,128)(2,1)S(1)} %pad_maximum_fusion.17), channel_id=1, source_target_pairs={{0,2},{2,4},{4,6},{1,3},{3,5},{5,7},{8,10},{10,12},{12,14},{9,11},... | collective-permute-start | bytes 9224 | tf_op jit(solution)/shard_map/ppermute | solution.py:12
  50.2 12.6 %collective-permute-start.28 = (bf16[32,3,3,1]{0,3,2,1:T(2,128)(2,1)S(1)}, bf16[32,3,3,1]{0,3,2,1:T(2,128)(2,1)S(1)}, u32[]{:S(2)}, u32[]{:S(2)}) collective-permute-start(bf16[32,3,3,1]{0,3,2,1:T(2,128)(2,1)S(1)} %get-tuple-element.49), channel_id=1, source_target_pairs={{0,1},{2,3},{4,5},{6,7},{8,9},{10,11},{12,13},{14,15},{16,17},{18,... | collective-permute-start | bytes 1736 | tf_op jit(solution)/shard_map/ppermute | solution.py:12
  51.5 11.3 %collective-permute-start.29 = (bf16[32,3,3,1]{0,3,2,1:T(2,128)(2,1)S(1)}, bf16[32,3,3,1]{0,3,2,1:T(2,128)(2,1)S(1)}, u32[]{:S(2)}, u32[]{:S(2)}) collective-permute-start(bf16[32,3,3,1]{0,3,2,1:T(2,128)(2,1)S(1)} %get-tuple-element.50), channel_id=1, source_target_pairs={{1,0},{3,2},{5,4},{7,6},{9,8},{11,10},{13,12},{15,14},{17,16},{19,... | collective-permute-start | bytes 1736 | tf_op jit(solution)/shard_map/ppermute | solution.py:15
  56.0 6.9 %collective-permute-start.14 = (bf16[32,4,1,32]{0,3,2,1:T(8,128)(2,1)S(1)}, bf16[32,4,1,32]{0,3,2,1:T(8,128)(2,1)S(1)}, u32[]{:S(2)}, u32[]{:S(2)}) collective-permute-start(bf16[32,4,1,32]{0,3,2,1:T(8,128)(2,1)S(1)} %get-tuple-element.45), channel_id=1, source_target_pairs={{0,2},{2,4},{4,6},{1,3},{3,5},{5,7},{8,10},{10,12},{12,14},{9,11},... | collective-permute-start | bytes 24584 | tf_op jit(solution)/shard_map/ppermute | solution.py:12
  57.9 5.9 %collective-permute-start.15 = (bf16[32,4,1,32]{0,3,2,1:T(8,128)(2,1)S(1)}, bf16[32,4,1,32]{0,3,2,1:T(8,128)(2,1)S(1)}, u32[]{:S(2)}, u32[]{:S(2)}) collective-permute-start(bf16[32,4,1,32]{0,3,2,1:T(8,128)(2,1)S(1)} %get-tuple-element.46), channel_id=1, source_target_pairs={{2,0},{4,2},{6,4},{3,1},{5,3},{7,5},{10,8},{12,10},{14,12},{11,9},... | collective-permute-start | bytes 24584 | tf_op jit(solution)/shard_map/ppermute | solution.py:15
  78.0 12.1 %collective-permute-start.32 = (bf16[32,4,1,32]{0,2,3,1:T(2,128)(2,1)S(1)}, bf16[32,4,1,32]{0,2,3,1:T(2,128)(2,1)S(1)}, u32[]{:S(2)}, u32[]{:S(2)}) collective-permute-start(bf16[32,4,1,32]{0,2,3,1:T(2,128)(2,1)S(1)} %get-tuple-element.43), channel_id=1, source_target_pairs={{0,2},{2,4},{4,6},{1,3},{3,5},{5,7},{8,10},{10,12},{12,14},{9,11},... | collective-permute-start | bytes 24584 | tf_op jit(solution)/shard_map/ppermute | solution.py:12
  79.9 10.2 %collective-permute-start.33 = (bf16[32,4,1,32]{0,2,3,1:T(2,128)(2,1)S(1)}, bf16[32,4,1,32]{0,2,3,1:T(2,128)(2,1)S(1)}, u32[]{:S(2)}, u32[]{:S(2)}) collective-permute-start(bf16[32,4,1,32]{0,2,3,1:T(2,128)(2,1)S(1)} %get-tuple-element.44), channel_id=1, source_target_pairs={{2,0},{4,2},{6,4},{3,1},{5,3},{7,5},{10,8},{12,10},{14,12},{11,9},... | collective-permute-start | bytes 24584 | tf_op jit(solution)/shard_map/ppermute | solution.py:15
  84.8 11.2 %collective-permute-start.6 = (bf16[32,1,4,64]{0,3,2,1:T(8,128)(2,1)S(1)}, bf16[32,1,4,64]{0,3,2,1:T(8,128)(2,1)S(1)}, u32[]{:S(2)}, u32[]{:S(2)}) collective-permute-start(bf16[32,1,4,64]{0,3,2,1:T(8,128)(2,1)S(1)} %get-tuple-element.35), channel_id=1, source_target_pairs={{0,8},{8,16},{16,24},{1,9},{9,17},{17,25},{2,10},{10,18},{18,26},{... | collective-permute-start | bytes 49160 | tf_op jit(solution)/shard_map/ppermute | solution.py:12
  86.7 9.3 %collective-permute-start.7 = (bf16[32,1,4,64]{0,3,2,1:T(8,128)(2,1)S(1)}, bf16[32,1,4,64]{0,3,2,1:T(8,128)(2,1)S(1)}, u32[]{:S(2)}, u32[]{:S(2)}) collective-permute-start(bf16[32,1,4,64]{0,3,2,1:T(8,128)(2,1)S(1)} %get-tuple-element.36), channel_id=1, source_target_pairs={{8,0},{16,8},{24,16},{9,1},{17,9},{25,17},{10,2},{18,10},{26,18},{... | collective-permute-start | bytes 49160 | tf_op jit(solution)/shard_map/ppermute | solution.py:15
  90.1 12.1 %collective-permute-start.34 = (bf16[32,4,4,1]{0,2,3,1:T(4,128)(2,1)S(1)}, bf16[32,4,4,1]{0,2,3,1:T(4,128)(2,1)S(1)}, u32[]{:S(2)}, u32[]{:S(2)}) collective-permute-start(bf16[32,4,4,1]{0,2,3,1:T(4,128)(2,1)S(1)} %get-tuple-element.37), channel_id=1, source_target_pairs={{0,1},{2,3},{4,5},{6,7},{8,9},{10,11},{12,13},{14,15},{16,17},{18,... | collective-permute-start | bytes 3080 | tf_op jit(solution)/shard_map/ppermute | solution.py:12
  91.4 10.8 %collective-permute-start.35 = (bf16[32,4,4,1]{0,2,3,1:T(4,128)(2,1)S(1)}, bf16[32,4,4,1]{0,2,3,1:T(4,128)(2,1)S(1)}, u32[]{:S(2)}, u32[]{:S(2)}) collective-permute-start(bf16[32,4,4,1]{0,2,3,1:T(4,128)(2,1)S(1)} %get-tuple-element.38), channel_id=1, source_target_pairs={{1,0},{3,2},{5,4},{7,6},{9,8},{11,10},{13,12},{15,14},{17,16},{19,... | collective-permute-start | bytes 3080 | tf_op jit(solution)/shard_map/ppermute | solution.py:15
  96.0 7.3 %collective-permute-start.8 = (bf16[32,6,1,64]{0,3,2,1:T(8,128)(2,1)S(1)}, bf16[32,6,1,64]{0,3,2,1:T(8,128)(2,1)S(1)}, u32[]{:S(2)}, u32[]{:S(2)}) collective-permute-start(bf16[32,6,1,64]{0,3,2,1:T(8,128)(2,1)S(1)} %get-tuple-element.23), channel_id=1, source_target_pairs={{0,2},{2,4},{4,6},{1,3},{3,5},{5,7},{8,10},{10,12},{12,14},{9,11},... | collective-permute-start | bytes 73736 | tf_op jit(solution)/shard_map/ppermute | solution.py:12
  97.9 6.7 %collective-permute-start.9 = (bf16[32,6,1,64]{0,3,2,1:T(8,128)(2,1)S(1)}, bf16[32,6,1,64]{0,3,2,1:T(8,128)(2,1)S(1)}, u32[]{:S(2)}, u32[]{:S(2)}) collective-permute-start(bf16[32,6,1,64]{0,3,2,1:T(8,128)(2,1)S(1)} %get-tuple-element.24), channel_id=1, source_target_pairs={{2,0},{4,2},{6,4},{3,1},{5,3},{7,5},{10,8},{12,10},{14,12},{11,9},... | collective-permute-start | bytes 73736 | tf_op jit(solution)/shard_map/ppermute | solution.py:15
  113.9 11.9 %collective-permute-start.36 = (bf16[32,1,4,64]{0,2,3,1:T(4,128)(2,1)S(1)}, bf16[32,1,4,64]{0,2,3,1:T(4,128)(2,1)S(1)}, u32[]{:S(2)}, u32[]{:S(2)}) collective-permute-start(bf16[32,1,4,64]{0,2,3,1:T(4,128)(2,1)S(1)} %get-tuple-element.29), channel_id=1, source_target_pairs={{0,8},{8,16},{16,24},{1,9},{9,17},{17,25},{2,10},{10,18},{18,26},{... | collective-permute-start | bytes 49160 | tf_op jit(solution)/shard_map/ppermute | solution.py:12
  115.8 10.0 %collective-permute-start.37 = (bf16[32,1,4,64]{0,2,3,1:T(4,128)(2,1)S(1)}, bf16[32,1,4,64]{0,2,3,1:T(4,128)(2,1)S(1)}, u32[]{:S(2)}, u32[]{:S(2)}) collective-permute-start(bf16[32,1,4,64]{0,2,3,1:T(4,128)(2,1)S(1)} %get-tuple-element.30), channel_id=1, source_target_pairs={{8,0},{16,8},{24,16},{9,1},{17,9},{25,17},{10,2},{18,10},{26,18},{... | collective-permute-start | bytes 49160 | tf_op jit(solution)/shard_map/ppermute | solution.py:15
  119.3 14.4 %collective-permute-start = (bf16[32,1,8,128]{3,0,2,1:T(8,128)(2,1)S(1)}, bf16[32,1,8,128]{3,0,2,1:T(8,128)(2,1)S(1)}, u32[]{:S(2)}, u32[]{:S(2)}) collective-permute-start(bf16[32,1,8,128]{3,0,2,1:T(8,128)(2,1)S(1)} %copy.186), channel_id=1, source_target_pairs={{0,8},{8,16},{16,24},{1,9},{9,17},{17,25},{2,10},{10,18},{18,26},{... | collective-permute-start | bytes 196616 | tf_op jit(solution)/shard_map/ppermute | solution.py:12
  121.2 12.9 %collective-permute-start.1 = (bf16[32,1,8,128]{3,0,2,1:T(8,128)(2,1)S(1)}, bf16[32,1,8,128]{3,0,2,1:T(8,128)(2,1)S(1)}, u32[]{:S(2)}, u32[]{:S(2)}) collective-permute-start(bf16[32,1,8,128]{3,0,2,1:T(8,128)(2,1)S(1)} %copy.187), channel_id=1, source_target_pairs={{8,0},{16,8},{24,16},{9,1},{17,9},{25,17},{10,2},{18,10},{26,18},{... | collective-permute-start | bytes 196616 | tf_op jit(solution)/shard_map/ppermute | solution.py:15
  126.8 9.1 %collective-permute-start.38 = (bf16[32,6,1,64]{0,2,3,1:T(2,128)(2,1)S(1)}, bf16[32,6,1,64]{0,2,3,1:T(2,128)(2,1)S(1)}, u32[]{:S(2)}, u32[]{:S(2)}) collective-permute-start(bf16[32,6,1,64]{0,2,3,1:T(2,128)(2,1)S(1)} %get-tuple-element.21), channel_id=1, source_target_pairs={{0,2},{2,4},{4,6},{1,3},{3,5},{5,7},{8,10},{10,12},{12,14},{9,11},... | collective-permute-start | bytes 73736 | tf_op jit(solution)/shard_map/ppermute | solution.py:12
  128.7 8.1 %collective-permute-start.39 = (bf16[32,6,1,64]{0,2,3,1:T(2,128)(2,1)S(1)}, bf16[32,6,1,64]{0,2,3,1:T(2,128)(2,1)S(1)}, u32[]{:S(2)}, u32[]{:S(2)}) collective-permute-start(bf16[32,6,1,64]{0,2,3,1:T(2,128)(2,1)S(1)} %get-tuple-element.22), channel_id=1, source_target_pairs={{2,0},{4,2},{6,4},{3,1},{5,3},{7,5},{10,8},{12,10},{14,12},{11,9},... | collective-permute-start | bytes 73736 | tf_op jit(solution)/shard_map/ppermute | solution.py:15
  137.1 12.2 %collective-permute-start.40 = (bf16[32,6,6,1]{3,0,2,1:T(8,128)(2,1)S(1)}, bf16[32,6,6,1]{3,0,2,1:T(8,128)(2,1)S(1)}, u32[]{:S(2)}, u32[]{:S(2)}) collective-permute-start(bf16[32,6,6,1]{3,0,2,1:T(8,128)(2,1)S(1)} %get-tuple-element.25), channel_id=1, source_target_pairs={{0,1},{2,3},{4,5},{6,7},{8,9},{10,11},{12,13},{14,15},{16,17},{18,... | collective-permute-start | bytes 6920 | tf_op jit(solution)/shard_map/ppermute | solution.py:12
  138.4 10.9 %collective-permute-start.41 = (bf16[32,6,6,1]{3,0,2,1:T(8,128)(2,1)S(1)}, bf16[32,6,6,1]{3,0,2,1:T(8,128)(2,1)S(1)}, u32[]{:S(2)}, u32[]{:S(2)}) collective-permute-start(bf16[32,6,6,1]{3,0,2,1:T(8,128)(2,1)S(1)} %get-tuple-element.26), channel_id=1, source_target_pairs={{1,0},{3,2},{5,4},{7,6},{9,8},{11,10},{13,12},{15,14},{17,16},{19,... | collective-permute-start | bytes 6920 | tf_op jit(solution)/shard_map/ppermute | solution.py:15
  142.4 10.0 %collective-permute-start.2 = (bf16[32,10,1,128]{3,0,2,1:T(8,128)(2,1)S(1)}, bf16[32,10,1,128]{3,0,2,1:T(8,128)(2,1)S(1)}, u32[]{:S(2)}, u32[]{:S(2)}) collective-permute-start(bf16[32,10,1,128]{3,0,2,1:T(8,128)(2,1)S(1)} %get-tuple-element.13), channel_id=1, source_target_pairs={{0,2},{2,4},{4,6},{1,3},{3,5},{5,7},{8,10},{10,12},{12,14},{9,11},... | collective-permute-start | bytes 245768 | tf_op jit(solution)/shard_map/ppermute | solution.py:12
  144.3 8.1 %collective-permute-start.3 = (bf16[32,10,1,128]{3,0,2,1:T(8,128)(2,1)S(1)}, bf16[32,10,1,128]{3,0,2,1:T(8,128)(2,1)S(1)}, u32[]{:S(2)}, u32[]{:S(2)}) collective-permute-start(bf16[32,10,1,128]{3,0,2,1:T(8,128)(2,1)S(1)} %get-tuple-element.14), channel_id=1, source_target_pairs={{2,0},{4,2},{6,4},{3,1},{5,3},{7,5},{10,8},{12,10},{14,12},{11,9},... | collective-permute-start | bytes 245768 | tf_op jit(solution)/shard_map/ppermute | solution.py:15
  154.5 15.5 %collective-permute-start.4 = (bf16[32,10,10,1]{0,2,3,1:T(8,128)(2,1)}, bf16[32,10,10,1]{0,2,3,1:T(8,128)(2,1)}, u32[]{:S(2)}, u32[]{:S(2)}) collective-permute-start(bf16[32,10,10,1]{0,2,3,1:T(8,128)(2,1)} %copy.123), channel_id=1, source_target_pairs={{0,1},{2,3},{4,5},{6,7},{8,9},{10,11},{12,13},{14,15},{16,17},{18,... | collective-permute-start | bytes 19208 | tf_op jit(solution)/shard_map/ppermute | solution.py:12
  157.5 14.1 %collective-permute-start.5 = (bf16[32,10,10,1]{0,2,3,1:T(8,128)(2,1)}, bf16[32,10,10,1]{0,2,3,1:T(8,128)(2,1)}, u32[]{:S(2)}, u32[]{:S(2)}) collective-permute-start(bf16[32,10,10,1]{0,2,3,1:T(8,128)(2,1)} %copy.124), channel_id=1, source_target_pairs={{1,0},{3,2},{5,4},{7,6},{9,8},{11,10},{13,12},{15,14},{17,16},{19,... | collective-permute-start | bytes 19208 | tf_op jit(solution)/shard_map/ppermute | solution.py:15
  (24 other events, 472.7 us)
where the time goes:
time: 212 us; the launch traced here: 209 us
  starting transfers between devices  120 us (57%)
  local copies, waits for them, and re-layouts  48.1 us (23%)
  waiting for transfers between devices  13.6 us (6%)
  matrix products  13.1 us (6%)
  other arithmetic  13 us (6%)
    ppermute x21, starting transfers between devices, padded_2(): lax.ppermute(lax.slice_in_dim(block, 0, width, axis=dim), axis, backward)  78.2 us
    ppermute x21, starting transfers between devices, padded_2(): lax.ppermute(lax.slice_in_dim(block, block.shape[dim] - width, None, axis...  42.3 us
    conv_general_dilated x14, local copies, waits for them, and re-layouts, conv_valid(): lax.conv_general_dilated(padded[None], kernel, (1, 1, 1), 'VALID', dimens...  20.8 us
    conv_general_dilated x4, matrix products, conv_valid(): lax.conv_general_dilated(padded[None], kernel, (1, 1, 1), 'VALID', dimens...  12.4 us
    ppermute x21, waiting for transfers between devices, padded_2(): lax.ppermute(lax.slice_in_dim(block, 0, width, axis=dim), axis, backward)  11.6 us
    reduce_sum x4, other arithmetic, restrict(): return jnp.mean(blocks, axis=(2, 4, 6)).astype(jnp.bfloat16)  5.33 us
    unnamed x37, local copies, waits for them, and re-layouts  5.2 us
    another operation x6, local copies, waits for them, and re-layouts, refine_padded(): joined = jnp.stack([even_cells, odd_cells], axis=dimension + 1)  4.24 us
  transfers between devices with their start and end apart: 42, of which 11 were waited for; matrix products, arithmetic and copies ran while one was open for 9% of the time, Pallas kernels for 0%

commit v1 on v0

v1 whole, which is shorter than its diff:
```python
import functools
import math

import jax
import jax.numpy as jnp
from jax import lax
from jax.experimental import pallas as pl
from jax.experimental.pallas import tpu as pltpu
from jax.sharding import PartitionSpec as P

F32 = jnp.float32
BF16 = jnp.bfloat16
MESH = pl.DeviceIdType.MESH


def iota(shape, dim):
    return lax.broadcasted_iota(jnp.int32, shape, dim)


def pair_sum(first, offset, lanes):
    source, target = iota((lanes, lanes), 0) - first, iota((lanes, lanes), 1) - offset
    return jnp.where(
        (source >= 0) & (target >= 0) & (lax.shift_right_arithmetic(source, 1) == target), 1.0, 0.0
    )


def spread(coarse_size, fine_shift, lanes):
    coarse = iota((lanes, lanes), 0) - 1
    fine = iota((lanes, lanes), 1) - fine_shift
    main = lax.shift_right_arithmetic(fine, 1)
    other = main + 2 * (fine & 1) - 1
    weight = jnp.where(coarse == main, 0.75, jnp.where(coarse == other, 0.25, 0.0))
    return jnp.where(coarse <= coarse_size, weight, 0.0).astype(BF16)


def dot(a, b):
    return jnp.dot(a, b, preferred_element_type=F32)


def kernel(counts, field, w0, wc, out, u0, uc, u3x, u3y, z0, zc, z3, v0, v1, v2, v3,
           zz1, zz2, zz3, qy0, send, recv):
    chans, bx, by, bz = field.shape
    cx, cy, cz = bx // 2, by // 2, bz // 2
    nx, ny, nz = counts
    gx, gy, gz = lax.axis_index("gx"), lax.axis_index("gy"), lax.axis_index("gz")
    place = {"gx": gx, "gy": gy, "gz": gz}
    size = {"gx": nx, "gy": ny, "gz": nz}
    reach = [("gx", d) for d in (-1, 1, -2, 2)] + [("gy", d) for d in (-1, 1, -2, 2)]
    reach += [("gz", -1), ("gz", 1)]

    def has(axis, d):
        target = place[axis] + d
        return (target >= 0) & (target < size[axis])

    def device(axis, d):
        where = dict(place)
        where[axis] = jnp.clip(place[axis] + d, 0, size[axis] - 1)
        return (where["gx"], where["gy"], where["gz"])

    for ref in (u0, uc, u3x, u3y, z0, zc, z3):
        ref[...] = jnp.zeros_like(ref)

    barrier = pltpu.get_barrier_semaphore()
    for axis, d in reach:
        if size[axis] > abs(d):
            @pl.when(has(axis, d))
            def _():
                pl.semaphore_signal(barrier, inc=1, device_id=device(axis, d), device_id_type=MESH)

    rows = chans * by
    perm_row, perm_col = iota((rows, rows), 0), iota((rows, rows), 1)
    perm = jnp.where(perm_col == (perm_row % chans) * by + perm_row // chans, 1.0, 0.0).astype(BF16)
    back = jnp.where(perm_row == (perm_col % chans) * by + perm_col // chans, 1.0, 0.0).astype(BF16)

    for x in range(bx):
        slab = field[:, x].astype(F32).reshape(rows, bz).astype(BF16)
        u0[1 + x, 1 : 1 + by] = dot(perm, slab).astype(BF16).reshape(by, chans, bz)

    def halve(blocks, matrix):
        stacked = jnp.concatenate(blocks, axis=0)
        summed = jnp.dot(stacked, matrix, precision=lax.Precision.HIGHEST, preferred_element_type=F32)
        rounded = (summed * 0.125).astype(BF16).astype(F32)
        return [rounded[chans * k : chans * (k + 1)] for k in range(len(blocks))]

    def quads(values, wide, high):
        return [
            values[2 * x * high + 2 * y] + values[(2 * x + 1) * high + 2 * y]
            + values[2 * x * high + 2 * y + 1] + values[(2 * x + 1) * high + 2 * y + 1]
            for x in range(wide // 2) for y in range(high // 2)
        ]

    fine = [u0[1 + x, 1 + y].astype(F32) for x in range(bx) for y in range(by)]
    first = halve(quads(fine, bx, by), pair_sum(0, 0, bz))
    second = halve(quads(first, cx, cy), pair_sum(0, cz, bz))
    third = halve(quads(second, cx // 2, cy // 2), pair_sum(cz, 0, bz))
    for x in range(cx):
        for y in range(cy):
            uc[2 + x, 2 + y] = (first[x * cy + y] + second[(x % 2) * (cy // 2) + y % 2]).astype(BF16)
    u3x[2] = third[0].astype(BF16)

    peers = sum(has(axis, d).astype(jnp.int32) for axis, d in reach)
    pl.semaphore_wait(barrier, peers)

    made = []

    def copy(axis, d, src, dst):
        k = len(made)
        made.append((axis, d))
        return axis, d, pltpu.make_async_remote_copy(
            src_ref=src, dst_ref=dst, send_sem=send.at[k], recv_sem=recv.at[k],
            device_id=device(axis, d), device_id_type=MESH)

    def start(copies):
        for axis, d, c in copies:
            if size[axis] > abs(d):
                @pl.when(has(axis, d))
                def _():
                    c.start()

    def arrive(copies):
        for axis, d, c in copies:
            if size[axis] > abs(d):
                @pl.when(has(axis, -d))
                def _():
                    c.wait_recv()

    def leave(copies):
        for axis, d, c in copies:
            if size[axis] > abs(d):
                @pl.when(has(axis, d))
                def _():
                    c.wait_send()

    own_y, own_cy = pl.ds(1, by), pl.ds(2, cy)
    x_small = [
        copy("gx", -1, uc.at[pl.ds(2, 2), own_cy], uc.at[pl.ds(cx + 2, 2), own_cy]),
        copy("gx", 1, uc.at[pl.ds(cx, 2), own_cy], uc.at[pl.ds(0, 2), own_cy]),
    ] + [copy("gx", d, u3x.at[2], u3x.at[2 - d]) for d in (-1, 1, -2, 2)]
    x_fine = [
        copy("gx", -1, u0.at[1, own_y], u0.at[bx + 1, own_y]),
        copy("gx", 1, u0.at[bx, own_y], u0.at[0, own_y]),
    ]
    y_small = [
        copy("gy", -1, uc.at[:, pl.ds(2, 2)], uc.at[:, pl.ds(cy + 2, 2)]),
        copy("gy", 1, uc.at[:, pl.ds(cy, 2)], uc.at[:, pl.ds(0, 2)]),
    ] + [copy("gy", d, u3y.at[2], u3y.at[2 - d]) for d in (-1, 1, -2, 2)]
    y_fine = [
        copy("gy", -1, u0.at[:, pl.ds(1, 1)], u0.at[:, pl.ds(by + 1, 1)]),
        copy("gy", 1, u0.at[:, pl.ds(by, 1)], u0.at[:, pl.ds(0, 1)]),
    ]
    z_small = [
        copy("gz", d, src, dst.at[(1 - d) // 2]) for d in (-1, 1) for src, dst in ((uc, zc), (u3y, z3))
    ]
    z_fine = [copy("gz", d, u0, z0.at[(1 - d) // 2]) for d in (-1, 1)]

    start(x_small)
    start(x_fine)
    arrive(x_small)
    width = bz // 8
    packed = u3x[0].astype(F32)
    for k in range(1, 5):
        packed = packed + pltpu.roll(u3x[k].astype(F32), k * width, 1)
    u3y[2] = packed.astype(BF16)
    start(y_small)
    arrive(x_fine)
    start(y_fine)
    arrive(y_small)
    start(z_small)
    arrive(y_fine)
    start(z_fine)
    arrive(z_small)

    lane = iota((chans, bz), 1)

    def roll(value, amount):
        amount = amount % bz
        return value if amount == 0 else pltpu.roll(value, amount, 1)

    def window(own, low, high, offset, length):
        own, low, high = own.astype(F32), low.astype(F32), high.astype(F32)
        value = jnp.where(lane < 2, roll(low, 2 - offset - length), 0.0)
        value = jnp.where((lane >= 2) & (lane < length + 2), roll(own, 2 - offset), value)
        value = jnp.where((lane >= length + 2) & (lane < length + 4), roll(high, length + 2 - offset), value)
        return jnp.concatenate([roll(value, -dz) for dz in range(3)], axis=0).astype(BF16)

    for k in range(5):
        for y in range(5):
            v3[k, y] = window(u3y[y], z3[0, y], z3[1, y], k * width, width)

    def fill2(x, carry):
        source_x = jnp.where(x >= 4, x + 2, x)
        for y in range(6):
            sy = y + 2 if y >= 4 else y
            v2[x, y] = window(uc[source_x, sy], zc[0, source_x, sy], zc[1, source_x, sy], cz, cz // 2)
        return carry

    lax.fori_loop(0, 6, fill2, 0)

    def fill1(x, carry):
        for y in range(cy + 4):
            v1[x, y] = window(uc[x, y], zc[0, x, y], zc[1, x, y], 0, cz)
        return carry

    lax.fori_loop(0, cx + 4, fill1, 0)

    depth = wc.shape[2]

    def patches(v, x, y):
        return jnp.concatenate(
            [v[x + dx, pl.ds(y, 3)].reshape(depth // 3, bz) for dx in range(3)], axis=0)

    def rim(length):
        low = jnp.where(gz > 0, 1.0, 0.0)
        high = jnp.where(gz < nz - 1, 1.0, 0.0)
        inside = jnp.where((lane >= 1) & (lane <= length), 1.0, 0.0)
        return inside + jnp.where(lane == 0, low, 0.0) + jnp.where(lane == length + 1, high, 0.0)

    def inside(index, length, axis):
        low = (index > 0) | (place[axis] > 0)
        high = (index <= length) | (place[axis] < size[axis] - 1)
        return jnp.where(low & high, 1.0, 0.0)

    rim3 = rim(width)
    w3 = wc[2]
    for x in range(3):
        for y in range(3):
            value = dot(w3, patches(v3, x, y))
            scale = inside(x, 1, "gx") * inside(y, 1, "gy")
            zz3[x, y] = (value * (rim3 * scale)).astype(BF16)

    def along_y(values, wide, shift):
        result = []
        for f in range(wide):
            cell = f - shift
            main = (cell >> 1) + 1
            other = main + 1 if cell & 1 else main - 1
            result.append(0.75 * values[main] + 0.25 * values[other])
        return result

    def raised(zz, coarse_size, shift):
        count_x, count_y = zz.shape[:2]
        spread_z = spread(coarse_size, shift, bz)
        flat = dot(zz[...].reshape(count_x * count_y * chans, bz), spread_z)
        return flat.reshape(count_x, count_y, chans, bz)

    def level(weights, v, zz, coarse, size_x, size_y, length, qy):
        mask = rim(length)
        for i in range((size_x + 2) // 2):
            for y in range(size_y + 2):
                value = dot(weights, jnp.concatenate(
                    [patches(v, 2 * i, y), patches(v, 2 * i + 1, y)], axis=1))
                a, b = qy[i][y], qy[i + 1][y]
                scale = mask * inside(y, size_y, "gy")
                zz[2 * i, y] = ((value[:, :bz] + 0.75 * a + 0.25 * b)
                                * (scale * inside(2 * i, size_x, "gx"))).astype(BF16)
                zz[2 * i + 1, y] = ((value[:, bz:] + 0.75 * b + 0.25 * a)
                                    * (scale * inside(2 * i + 1, size_x, "gx"))).astype(BF16)

    q3 = raised(zz3, width, 1)
    qy3 = [along_y([q3[x, y] for y in range(3)], 4, 1) for x in range(3)]
    level(wc[1], v2, zz2, zz3, cx // 2, cy // 2, cz // 2, qy3)
    q2 = raised(zz2, cz // 2, 1)
    qy2 = [along_y([q2[x, y] for y in range(cy // 2 + 2)], cy + 2, 1) for x in range(cx // 2 + 2)]
    level(wc[0], v1, zz1, zz2, cx, cy, cz, qy2)
    q1 = raised(zz1, cz, 0)
    for x in range(cx + 2):
        for y, value in enumerate(along_y([q1[x, y] for y in range(cy + 2)], by, 0)):
            qy0[x, y] = value

    arrive(z_fine)

    def fill0(x, carry):
        for y in range(by + 2):
            own = u0[x, y]
            wide = own.astype(F32)
            low = jnp.where(lane == bz - 1, z0[0, x, y].astype(F32), wide)
            high = jnp.where(lane == 0, z0[1, x, y].astype(F32), wide)
            v0[x, y] = jnp.concatenate([roll(low, 1).astype(BF16), own, roll(high, -1).astype(BF16)], axis=0)
        return carry

    lax.fori_loop(0, bx + 2, fill0, 0)

    weights = w0[...]
    scale = math.sqrt(2.0 / math.pi)

    def finish(i, carry):
        done = []
        for y in range(by):
            sides = [
                jnp.concatenate([patches(v0, 2 * i + k, y), u0[2 * i + k + 1, y + 1]], axis=0)
                for k in range(2)
            ]
            value = dot(weights, jnp.concatenate(sides, axis=1))
            a, b, c = qy0[i, y], qy0[i + 1, y], qy0[i + 2, y]
            value = value + jnp.concatenate([0.75 * b + 0.25 * a, 0.75 * b + 0.25 * c], axis=1)
            inner = scale * (value + 0.044715 * (value * value * value))
            done.append((0.5 * value * (1.0 + jnp.tanh(inner))).astype(BF16))
        whole = dot(back, jnp.concatenate(done, axis=0))
        for k in range(2):
            part = whole[:, k * bz : (k + 1) * bz].reshape(chans, by, bz).astype(BF16)
            out[:, pl.ds(2 * i + k, 1)] = part.reshape(chans, 1, by, bz)
        return carry

    lax.fori_loop(0, bx // 2, finish, 0)

    for group in (x_small, x_fine, y_small, y_fine, z_small, z_fine):
        leave(group)


def solution(mesh):
    counts = tuple(mesh.shape[axis] for axis in ("gx", "gy", "gz"))

    def on_device(field, mixing, kernel_fine, kernel_half, kernel_quarter, kernel_eighth):
        chans, bx, by, bz = field.shape
        cx, cy = bx // 2, by // 2
        w0 = jnp.concatenate([kernel_fine.reshape(-1, chans), mixing.T], axis=0).T
        wc = jnp.stack([k.reshape(-1, chans) for k in (kernel_half, kernel_quarter, kernel_eighth)])
        wc = wc.transpose(0, 2, 1)
        vmem = pl.BlockSpec(memory_space=pltpu.VMEM)

        def buf(*dims, dtype=BF16):
            return pltpu.VMEM(dims, dtype)

        fine = (bx + 2, by + 2, chans, bz)
        coarse = (cx + 4, cy + 4, chans, bz)
        return pl.pallas_call(
            functools.partial(kernel, counts),
            out_shape=jax.ShapeDtypeStruct(field.shape, BF16),
            in_specs=[vmem] * 3,
            out_specs=vmem,
            scratch_shapes=[
                buf(*fine), buf(*coarse), buf(5, chans, bz), buf(5, chans, bz),
                buf(2, *fine), buf(2, *coarse), buf(2, 5, chans, bz),
                buf(bx + 2, by + 2, 3 * chans, bz),
                buf(cx + 4, cy + 4, 3 * chans, bz),
                buf(6, 6, 3 * chans, bz), buf(5, 5, 3 * chans, bz),
                buf(cx + 2, cy + 2, chans, bz), buf(4, 4, chans, bz), buf(3, 3, chans, bz),
                buf(cx + 2, by, chans, bz, dtype=F32),
                pltpu.SemaphoreType.DMA((22,)), pltpu.SemaphoreType.DMA((22,)),
            ],
            compiler_params=pltpu.CompilerParams(
                collective_id=0, has_side_effects=True, vmem_limit_bytes=56 * 2**20),
        )(field, w0, wc)

    placed = (P(None, "gx", "gy", "gz"), P(), P(), P(), P(), P())
    return jax.shard_map(
        on_device, mesh=mesh, in_specs=placed, out_specs=P(None, "gx", "gy", "gz"), check_vma=False
    )
```

time: 212 us -> 38.5 us (0.18)
  the two profiles are of different devices: /device:TPU:13 before, /device:TPU:1 now
where the time goes in v1:
time: 38.5 us; the launch traced here: 38.3 us
  Pallas kernels  32.7 us (85%)
  local copies, waits for them, and re-layouts  4.07 us (11%)
  other arithmetic  1.4 us (4%)
    pallas_call x1, Pallas kernels, on_device(): pl.pallas_call(functools.partial(kernel, counts), out_shape=jax.ShapeDtyp...  32.7 us
    unnamed x9, local copies, waits for them, and re-layouts  2.58 us
    reshape x1, local copies, waits for them, and re-layouts, on_device(): w0 = jnp.concatenate([kernel_fine.reshape(-1, chans), mixing.T], axis=0).T  1.11 us

profile of v1, /device:TPU:1, one launch (start us, length us, event | category | flops | bytes accessed | tf_op | source)
XLA Modules:
  0.0 38.3 jit_solution(9107424013318015103)
XLA Ops:
  0.0 0.0 copy-start
  0.0 0.0 copy-start.3
  0.0 1.1 %copy.15 = bf16[864,32]{0,1:T(8,128)(2,1)S(1)} copy(bf16[864,32]{1,0:T(8,128)(2,1)} %bitcast.9) | data formatting | bytes 110592 | tf_op jit(solution)/shard_map/reshape | solution.py:316
  1.1 0.0 copy-done.3
  1.1 0.0 copy-start.1
  1.1 0.7 %maximum_bitcast_fusion.1.w0 = bf16[32,896]{1,0:T(8,128)(2,1)} fusion(bf16[32,32]{0,1:T(8,128)(2,1)S(1)} %bitcast.13, bf16[864,32]{0,1:T(8,128)(2,1)S(1)} %copy.15), kind=kLoop, calls=%fused_computation.1 | loop fusion | flops 114688 | bytes 114688 | tf_op jit(solution)/shard_map/transpose | solution.py:316
  1.8 0.0 copy-done
  1.8 0.0 copy-start.2
  1.8 0.1 copy.16
  2.0 0.1 copy-done.1
  2.1 0.1 copy.17
  2.2 0.6 %copy-done.2 = bf16[3,3,3,32,32]{4,3,2,1,0:T(8,128)(2,1)S(1)} copy-done((bf16[3,3,3,32,32]{4,3,2,1,0:T(8,128)(2,1)S(1)}, bf16[3,3,3,32,32]{4,3,2,1,0:T(8,128)(2,1)}, u32[]{:S(2)}) %copy-start.2) | copy-done | bytes 55320
  2.8 0.1 copy.18
  2.9 0.7 %maximum_bitcast_fusion.wc = bf16[3,32,864]{2,1,0:T(8,128)(2,1)} fusion(bf16[1,864,32]{1,2,0:T(8,128)(2,1)S(1)} %copy.18, bf16[1,864,32]{1,2,0:T(8,128)(2,1)S(1)} %copy.17, bf16[1,864,32]{1,2,0:T(8,128)(2,1)S(1)} %copy.16), kind=kLoop, calls=%fused_computation | loop fusion | flops 165888 | bytes 331776 | tf_op jit(solution)/shard_map/transpose | solution.py:318
  3.6 32.7 %shard_map.64 = bf16[32,8,8,128]{3,2,1,0:T(8,128)(2,1)} custom-call(bf16[32,8,8,128]{3,2,1,0:T(8,128)(2,1)} %field.1, bf16[32,896]{1,0:T(8,128)(2,1)} %maximum_bitcast_fusion.1.w0, bf16[3,32,864]{2,1,0:T(8,128)(2,1)} %maximum_bitcast_fusion.wc), custom_call_target="tpu_custom_call" | custom-call | tf_op jit(solution)/shard_map/pallas_call | solution.py:326
  36.4 1.9 %copy.20 = bf16[32,8,8,128]{3,2,1,0:T(8,128)(2,1)} copy(bf16[32,8,8,128]{3,2,1,0:T(8,128)(2,1)} %shard_map.64) | data formatting | bytes 1048576
Async XLA Ops:
  0.0 1.8 %copy-start = (bf16[3,3,3,32,32]{4,3,2,1,0:T(8,128)(2,1)S(1)}, bf16[3,3,3,32,32]{4,3,2,1,0:T(8,128)(2,1)}, u32[]{:S(2)}) copy-start(bf16[3,3,3,32,32]{4,3,2,1,0:T(8,128)(2,1)} %param.9) | copy-start | bytes 165892
  0.0 1.1 %copy-start.3 = (bf16[32,32]{1,0:T(8,128)(2,1)S(1)}, bf16[32,32]{1,0:T(8,128)(2,1)}, u32[]{:S(2)}) copy-start(bf16[32,32]{1,0:T(8,128)(2,1)} %param.7) | copy-start | bytes 6148
  1.1 0.9 %copy-start.1 = (bf16[3,3,3,32,32]{4,3,2,1,0:T(8,128)(2,1)S(1)}, bf16[3,3,3,32,32]{4,3,2,1,0:T(8,128)(2,1)}, u32[]{:S(2)}) copy-start(bf16[3,3,3,32,32]{4,3,2,1,0:T(8,128)(2,1)} %param.10) | copy-start | bytes 165892
  1.8 1.0 %copy-start.2 = (bf16[3,3,3,32,32]{4,3,2,1,0:T(8,128)(2,1)S(1)}, bf16[3,3,3,32,32]{4,3,2,1,0:T(8,128)(2,1)}, u32[]{:S(2)}) copy-start(bf16[3,3,3,32,32]{4,3,2,1,0:T(8,128)(2,1)} %param.11) | copy-start | bytes 165892

commit v2 on v1

--- a/solution.py
+++ b/solution.py
@@ -37,35 +37,56 @@
     return jnp.dot(a, b, preferred_element_type=F32)
 
 
-def kernel(counts, field, w0, wc, out, u0, uc, u3x, u3y, z0, zc, z3, v0, v1, v2, v3,
-           zz1, zz2, zz3, qy0, send, recv):
+def kernel(counts, field, mixing, raw_fine, raw_half, raw_quarter, raw_eighth, out, u0, uc, u3x, u3y,
+           z0, zc, z3, v0, v1, v2, v3, zz1, zz2, zz3, qy0, y0, raw, wall, send, recv, loaded):
     chans, bx, by, bz = field.shape
     cx, cy, cz = bx // 2, by // 2, bz // 2
-    nx, ny, nz = counts
-    gx, gy, gz = lax.axis_index("gx"), lax.axis_index("gy"), lax.axis_index("gz")
-    place = {"gx": gx, "gy": gy, "gz": gz}
-    size = {"gx": nx, "gy": ny, "gz": nz}
-    reach = [("gx", d) for d in (-1, 1, -2, 2)] + [("gy", d) for d in (-1, 1, -2, 2)]
-    reach += [("gz", -1), ("gz", 1)]
-
-    def has(axis, d):
-        target = place[axis] + d
-        return (target >= 0) & (target < size[axis])
-
-    def device(axis, d):
-        where = dict(place)
-        where[axis] = jnp.clip(place[axis] + d, 0, size[axis] - 1)
-        return (where["gx"], where["gy"], where["gz"])
-
-    for ref in (u0, uc, u3x, u3y, z0, zc, z3):
+    taps = raw_fine.shape[0]
+    place = {axis: lax.axis_index(axis) for axis in ("gx", "gy", "gz")}
+    size = dict(zip(("gx", "gy", "gz"), counts))
+    axes = ("gx", "gy", "gz")
+    gz, nz = place["gz"], size["gz"]
+    reach = [(d, 0, 0) for d in (-1, 1, -2, 2)] + [(0, d, 0) for d in (-1, 1, -2, 2)]
+    reach += [(a, b, 0) for a in (-1, 1) for b in (-1, 1)] + [(0, 0, -1), (0, 0, 1)]
+
+    def possible(d):
+        return all(size[axis] > abs(k) for axis, k in zip(axes, d))
+
+    def has(d):
+        found = True
+        for axis, k in zip(axes, d):
+            if k:
+                found = found & (place[axis] + k >= 0) & (place[axis] + k < size[axis])
+        return found
+
+    def device(d):
+        return tuple(jnp.clip(place[axis] + k, 0, size[axis] - 1) for axis, k in zip(axes, d))
+
+    loads = [
+        pltpu.make_async_copy(source, raw.at[k], loaded.at[k])
+        for k, source in enumerate((raw_fine, raw_half, raw_quarter, raw_eighth))
+    ]
+    for load in loads:
+        load.start()
+
+    for ref in (uc, u3x, u3y):
         ref[...] = jnp.zeros_like(ref)
+    for x in (0, bx + 1):
+        u0[x] = jnp.zeros((by + 2, chans, bz), BF16)
+    for y in (0, by + 1):
+        u0[pl.ds(1, bx), y] = jnp.zeros((bx, chans, bz), BF16)
+    for side, d in ((0, -1), (1, 1)):
+        @pl.when(jnp.logical_not(has((0, 0, d))))
+        def _():
+            for ref in (z0, zc, z3):
+                ref[side] = jnp.zeros(ref.shape[1:], BF16)
 
     barrier = pltpu.get_barrier_semaphore()
-    for axis, d in reach:
-        if size[axis] > abs(d):
-            @pl.when(has(axis, d))
+    for d in reach:
+        if possible(d):
+            @pl.when(has(d))
             def _():
-                pl.semaphore_signal(barrier, inc=1, device_id=device(axis, d), device_id_type=MESH)
+                pl.semaphore_signal(barrier, inc=1, device_id=device(d), device_id_type=MESH)
 
     rows = chans * by
     perm_row, perm_col = iota((rows, rows), 0), iota((rows, rows), 1)
@@ -98,77 +119,104 @@
             uc[2 + x, 2 + y] = (first[x * cy + y] + second[(x % 2) * (cy // 2) + y % 2]).astype(BF16)
     u3x[2] = third[0].astype(BF16)
 
-    peers = sum(has(axis, d).astype(jnp.int32) for axis, d in reach)
+    peers = sum(has(d).astype(jnp.int32) for d in reach if possible(d))
     pl.semaphore_wait(barrier, peers)
 
     made = []
 
-    def copy(axis, d, src, dst):
+    def copy(d, src, dst):
         k = len(made)
-        made.append((axis, d))
-        return axis, d, pltpu.make_async_remote_copy(
+        made.append(d)
+        return d, pltpu.make_async_remote_copy(
             src_ref=src, dst_ref=dst, send_sem=send.at[k], recv_sem=recv.at[k],
-            device_id=device(axis, d), device_id_type=MESH)
+            device_id=device(d), device_id_type=MESH)
 
     def start(copies):
-        for axis, d, c in copies:
-            if size[axis] > abs(d):
-                @pl.when(has(axis, d))
+        for d, c in copies:
+            if possible(d):
+                @pl.when(has(d))
                 def _():
                     c.start()
 
     def arrive(copies):
-        for axis, d, c in copies:
-            if size[axis] > abs(d):
-                @pl.when(has(axis, -d))
+        for d, c in copies:
+            if possible(d):
+                @pl.when(has(tuple(-k for k in d)))
                 def _():
                     c.wait_recv()
 
     def leave(copies):
-        for axis, d, c in copies:
-            if size[axis] > abs(d):
-                @pl.when(has(axis, d))
+        for d, c in copies:
+            if possible(d):
+                @pl.when(has(d))
                 def _():
                     c.wait_send()
 
-    own_y, own_cy = pl.ds(1, by), pl.ds(2, cy)
-    x_small = [
-        copy("gx", -1, uc.at[pl.ds(2, 2), own_cy], uc.at[pl.ds(cx + 2, 2), own_cy]),
-        copy("gx", 1, uc.at[pl.ds(cx, 2), own_cy], uc.at[pl.ds(0, 2), own_cy]),
-    ] + [copy("gx", d, u3x.at[2], u3x.at[2 - d]) for d in (-1, 1, -2, 2)]
-    x_fine = [
-        copy("gx", -1, u0.at[1, own_y], u0.at[bx + 1, own_y]),
-        copy("gx", 1, u0.at[bx, own_y], u0.at[0, own_y]),
-    ]
-    y_small = [
-        copy("gy", -1, uc.at[:, pl.ds(2, 2)], uc.at[:, pl.ds(cy + 2, 2)]),
-        copy("gy", 1, uc.at[:, pl.ds(cy, 2)], uc.at[:, pl.ds(0, 2)]),
-    ] + [copy("gy", d, u3y.at[2], u3y.at[2 - d]) for d in (-1, 1, -2, 2)]
-    y_fine = [
-        copy("gy", -1, u0.at[:, pl.ds(1, 1)], u0.at[:, pl.ds(by + 1, 1)]),
-        copy("gy", 1, u0.at[:, pl.ds(by, 1)], u0.at[:, pl.ds(0, 1)]),
-    ]
-    z_small = [
-        copy("gz", d, src, dst.at[(1 - d) // 2]) for d in (-1, 1) for src, dst in ((uc, zc), (u3y, z3))
-    ]
-    z_fine = [copy("gz", d, u0, z0.at[(1 - d) // 2]) for d in (-1, 1)]
-
-    start(x_small)
-    start(x_fine)
-    arrive(x_small)
+    def spans(d, length, depth):
+        if d == 0:
+            return depth, depth, length
+        return (depth, length + depth, depth) if d < 0 else (length, 0, depth)
+
+    def rims(ref, length_x, length_y, depth):
+        result = []
+        for dx in (-1, 0, 1):
+            for dy in (-1, 0, 1):
+                if dx or dy:
+                    sx, tx, wx = spans(dx, length_x, depth)
+                    sy, ty, wy = spans(dy, length_y, depth)
+                    result.append(copy((dx, dy, 0), ref.at[pl.ds(sx, wx), pl.ds(sy, wy)],
+                                       ref.at[pl.ds(tx, wx), pl.ds(ty, wy)]))
+        return result
+
+    def across(ref, dst, pieces):
+        return [
+            copy((0, 0, d), ref.at[piece], dst.at[((1 - d) // 2,) + piece])
+            for d in (-1, 1) for piece in pieces
+        ]
+
+    def frame(length_x, length_y, depth):
+        whole_y = pl.ds(0, length_y + 2 * depth)
+        mid_x = pl.ds(depth, length_x)
+        return [
+            (pl.ds(0, depth), whole_y), (pl.ds(length_x + depth, depth), whole_y),
+            (mid_x, pl.ds(0, depth)), (mid_x, pl.ds(length_y + depth, depth)),
+        ]
+
+    x_last = [copy((d, 0, 0), u3x.at[2], u3x.at[2 - d]) for d in (-1, 1, -2, 2)]
+    y_last = [copy((0, d, 0), u3y.at[2], u3y.at[2 - d]) for d in (-1, 1, -2, 2)]
+    z_last = [copy((0, 0, d), u3y, z3.at[(1 - d) // 2]) for d in (-1, 1)]
+    small = rims(uc, cx, cy, 2)
+    fine_rims = rims(u0, bx, by, 1)
+    z_own = across(uc, zc, [(pl.ds(2, cx), pl.ds(2, cy))])
+    z_own_fine = across(u0, z0, [(pl.ds(1, bx), pl.ds(1, by))])
+    z_small = across(uc, zc, frame(cx, cy, 2))
+    z_fine = across(u0, z0, frame(bx, by, 1))
+
+    start(x_last)
+    start(small)
+    start(z_own_fine)
+    start(z_own)
+    start(fine_rims)
+
+    eye = jnp.where(iota((chans, chans), 0) == iota((chans, chans), 1), 1.0, 0.0).astype(BF16)
+
+    def turned(value):
+        return lax.dot_general(eye, value, (((1,), (1,)), ((), ())), preferred_element_type=F32).astype(BF16)
+
+    for load in loads:
+        load.wait()
+    fine_rows = jnp.concatenate([raw[0], turned(mixing[...])], axis=0)
+    wall[0] = turned(fine_rows)
+    for k in range(1, 4):
+        wall[k, :, pl.ds(0, taps)] = turned(raw[k])
+
+    arrive(x_last)
     width = bz // 8
     packed = u3x[0].astype(F32)
     for k in range(1, 5):
         packed = packed + pltpu.roll(u3x[k].astype(F32), k * width, 1)
     u3y[2] = packed.astype(BF16)
-    start(y_small)
-    arrive(x_fine)
-    start(y_fine)
-    arrive(y_small)
-    start(z_small)
-    arrive(y_fine)
-    start(z_fine)
-    arrive(z_small)
+    start(y_last)
 
     lane = iota((chans, bz), 1)
 
@@ -183,6 +231,52 @@
         value = jnp.where((lane >= length + 2) & (lane < length + 4), roll(high, length + 2 - offset), value)
         return jnp.concatenate([roll(value, -dz) for dz in range(3)], axis=0).astype(BF16)
 
+    def fill_fine(x, y):
+        own = u0[x, y]
+        wide = own.astype(F32)
+        low = jnp.where(lane == bz - 1, z0[0, x, y].astype(F32), wide)
+        high = jnp.where(lane == 0, z0[1, x, y].astype(F32), wide)
+        v0[x, y] = jnp.concatenate([roll(low, 1).astype(BF16), own, roll(high, -1).astype(BF16)], axis=0)
+
+    def patches(v, x, y):
+        return jnp.concatenate(
+            [v[x + dx, pl.ds(y, 3)].reshape(taps // 3, bz) for dx in range(3)], axis=0)
+
+    weights = wall[0]
+
+    def fine_pair(xa, xb, y):
+        sides = [jnp.concatenate([patches(v0, x, y), u0[x + 1, y + 1]], axis=0) for x in (xa, xb)]
+        value = dot(weights, jnp.concatenate(sides, axis=1))
+        y0[xa, y] = value[:, :bz]
+        y0[xb, y] = value[:, bz:]
+
+    arrive(z_own_fine)
+
+    def fill_own(x, carry):
+        for y in range(by):
+            fill_fine(x + 1, y + 1)
+        return carry
+
+    lax.fori_loop(0, bx, fill_own, 0)
+
+    arrive(small)
+    start(z_small)
+    arrive(y_last)
+    start(z_last)
+    arrive(fine_rims)
+    start(z_fine)
+
+    def interior(p, carry):
+        for y in range(1, by - 1):
+            fine_pair(1 + 2 * p, 2 + 2 * p, y)
+        return carry
+
+    lax.fori_loop(0, (bx - 2) // 2, interior, 0)
+
+    arrive(z_own)
+    arrive(z_small)
+    arrive(z_last)
+
     for k in range(5):
         for y in range(5):
             v3[k, y] = window(u3y[y], z3[0, y], z3[1, y], k * width, width)
@@ -203,12 +297,6 @@
 
     lax.fori_loop(0, cx + 4, fill1, 0)
 
-    depth = wc.shape[2]
-
-    def patches(v, x, y):
-        return jnp.concatenate(
-            [v[x + dx, pl.ds(y, 3)].reshape(depth // 3, bz) for dx in range(3)], axis=0)
-
     def rim(length):
         low = jnp.where(gz > 0, 1.0, 0.0)
         high = jnp.where(gz < nz - 1, 1.0, 0.0)
@@ -221,7 +309,7 @@
         return jnp.where(low & high, 1.0, 0.0)
 
     rim3 = rim(width)
-    w3 = wc[2]
+    w3 = wall[3, :, pl.ds(0, taps)]
     for x in range(3):
         for y in range(3):
             value = dot(w3, patches(v3, x, y))
@@ -258,10 +346,10 @@
 
     q3 = raised(zz3, width, 1)
     qy3 = [along_y([q3[x, y] for y in range(3)], 4, 1) for x in range(3)]
-    level(wc[1], v2, zz2, zz3, cx // 2, cy // 2, cz // 2, qy3)
+    level(wall[2, :, pl.ds(0, taps)], v2, zz2, zz3, cx // 2, cy // 2, cz // 2, qy3)
     q2 = raised(zz2, cz // 2, 1)
     qy2 = [along_y([q2[x, y] for y in range(cy // 2 + 2)], cy + 2, 1) for x in range(cx // 2 + 2)]
-    level(wc[0], v1, zz1, zz2, cx, cy, cz, qy2)
+    level(wall[1, :, pl.ds(0, taps)], v1, zz1, zz2, cx, cy, cz, qy2)
     q1 = raised(zz1, cz, 0)
     for x in range(cx + 2):
         for y, value in enumerate(along_y([q1[x, y] for y in range(cy + 2)], by, 0)):
@@ -269,30 +357,38 @@
 
     arrive(z_fine)
 
-    def fill0(x, carry):
-        for y in range(by + 2):
-            own = u0[x, y]
-            wide = own.astype(F32)
-            low = jnp.where(lane == bz - 1, z0[0, x, y].astype(F32), wide)
-            high = jnp.where(lane == 0, z0[1, x, y].astype(F32), wide)
-            v0[x, y] = jnp.concatenate([roll(low, 1).astype(BF16), own, roll(high, -1).astype(BF16)], axis=0)
-        return carry
-
-    lax.fori_loop(0, bx + 2, fill0, 0)
-
-    weights = w0[...]
+    def fill_rows(y, carry):
+        for x in (0, bx + 1):
+            fill_fine(x, y)
+        return carry
+
+    lax.fori_loop(0, by + 2, fill_rows, 0)
+
+    def fill_columns(x, carry):
+        for y in (0, by + 1):
+            fill_fine(x + 1, y)
+        return carry
+
+    lax.fori_loop(0, bx, fill_columns, 0)
+
+    for y in range(by):
+        fine_pair(0, bx - 1, y)
+
+    def edges(p, carry):
+        for y in (0, by - 1):
+            fine_pair(1 + 2 * p, 2 + 2 * p, y)
+        return carry
+
+    lax.fori_loop(0, (bx - 2) // 2, edges, 0)
+
     scale = math.sqrt(2.0 / math.pi)
 
     def finish(i, carry):
         done = []
         for y in range(by):
-            sides = [
-                jnp.concatenate([patches(v0, 2 * i + k, y), u0[2 * i + k + 1, y + 1]], axis=0)
-                for k in range(2)
-            ]
-            value = dot(weights, jnp.concatenate(sides, axis=1))
             a, b, c = qy0[i, y], qy0[i + 1, y], qy0[i + 2, y]
-            value = value + jnp.concatenate([0.75 * b + 0.25 * a, 0.75 * b + 0.25 * c], axis=1)
+            value = jnp.concatenate(
+                [y0[2 * i, y] + (0.75 * b + 0.25 * a), y0[2 * i + 1, y] + (0.75 * b + 0.25 * c)], axis=1)
             inner = scale * (value + 0.044715 * (value * value * value))
             done.append((0.5 * value * (1.0 + jnp.tanh(inner))).astype(BF16))
         whole = dot(back, jnp.concatenate(done, axis=0))
@@ -303,20 +399,20 @@
 
     lax.fori_loop(0, bx // 2, finish, 0)
 
-    for group in (x_small, x_fine, y_small, y_fine, z_small, z_fine):
+    for group in (x_last, small, z_own_fine, z_own, fine_rims, y_last, z_small, z_last, z_fine):
         leave(group)
 
 
 def solution(mesh):
     counts = tuple(mesh.shape[axis] for axis in ("gx", "gy", "gz"))
 
-    def on_device(field, mixing, kernel_fine, kernel_half, kernel_quarter, kernel_eighth):
+    def on_device(field, mixing, *kernels):
         chans, bx, by, bz = field.shape
         cx, cy = bx // 2, by // 2
-        w0 = jnp.concatenate([kernel_fine.reshape(-1, chans), mixing.T], axis=0).T
-        wc = jnp.stack([k.reshape(-1, chans) for k in (kernel_half, kernel_quarter, kernel_eighth)])
-        wc = wc.transpose(0, 2, 1)
+        rows = [k.reshape(-1, chans) for k in kernels]
+        taps = rows[0].shape[0]
         vmem = pl.BlockSpec(memory_space=pltpu.VMEM)
+        anywhere = pl.BlockSpec(memory_space=pl.ANY)
 
         def buf(*dims, dtype=BF16):
             return pltpu.VMEM(dims, dtype)
@@ -326,7 +422,7 @@
         return pl.pallas_call(
             functools.partial(kernel, counts),
             out_shape=jax.ShapeDtypeStruct(field.shape, BF16),
-            in_specs=[vmem] * 3,
+            in_specs=[vmem] * 2 + [anywhere] * 4,
             out_specs=vmem,
             scratch_shapes=[
                 buf(*fine), buf(*coarse), buf(5, chans, bz), buf(5, chans, bz),
@@ -335,12 +431,14 @@
                 buf(cx + 4, cy + 4, 3 * chans, bz),
                 buf(6, 6, 3 * chans, bz), buf(5, 5, 3 * chans, bz),
                 buf(cx + 2, cy + 2, chans, bz), buf(4, 4, chans, bz), buf(3, 3, chans, bz),
-                buf(cx + 2, by, chans, bz, dtype=F32),
-                pltpu.SemaphoreType.DMA((22,)), pltpu.SemaphoreType.DMA((22,)),
+                buf(cx + 2, by, chans, bz, dtype=F32), buf(bx, by, chans, bz, dtype=F32),
+                buf(4, taps, chans), buf(4, chans, taps + chans),
+                pltpu.SemaphoreType.DMA((48,)), pltpu.SemaphoreType.DMA((48,)),
+                pltpu.SemaphoreType.DMA((4,)),
             ],
             compiler_params=pltpu.CompilerParams(
-                collective_id=0, has_side_effects=True, vmem_limit_bytes=56 * 2**20),
-        )(field, w0, wc)
+                collective_id=0, has_side_effects=True, vmem_limit_bytes=24 * 2**20),
+        )(field, mixing, *rows)
 
     placed = (P(None, "gx", "gy", "gz"), P(), P(), P(), P(), P())
     return jax.shard_map(

time: 38.5 us -> 35.5 us (0.922)
  the two profiles are of different devices: /device:TPU:1 before, /device:TPU:12 now
where the time goes in v2:
time: 35.5 us; the launch traced here: 35.2 us
  Pallas kernels  28.9 us (81%)
  local copies, waits for them, and re-layouts  6.27 us (18%)
    pallas_call x1, Pallas kernels, on_device(): pl.pallas_call(functools.partial(kernel, counts), out_shape=jax.ShapeDtyp...  28.9 us
    unnamed x13, local copies, waits for them, and re-layouts  6.27 us

profile of v2, /device:TPU:12, one launch (start us, length us, event | category | flops | bytes accessed | tf_op | source)
XLA Modules:
  0.0 35.2 jit_solution(16273087291202827597)
XLA Ops:
  0.0 0.0 copy-start
  0.0 1.0 %copy-done = bf16[32,8,8,128]{3,2,1,0:T(8,128)(2,1)S(1)} copy-done((bf16[32,8,8,128]{3,2,1,0:T(8,128)(2,1)S(1)}, bf16[32,8,8,128]{3,2,1,0:T(8,128)(2,1)}, u32[]{:S(2)}) %copy-start) | copy-done | bytes 524312
  1.0 0.0 copy-start.1
  1.0 0.9 %copy-done.1 = bf16[3,3,3,32,32]{4,3,2,1,0:T(8,128)(2,1)S(1)} copy-done((bf16[3,3,3,32,32]{4,3,2,1,0:T(8,128)(2,1)S(1)}, bf16[3,3,3,32,32]{4,3,2,1,0:T(8,128)(2,1)}, u32[]{:S(2)}) %copy-start.1) | copy-done | bytes 55320
  2.0 0.0 copy-start.2
  2.0 0.9 %copy-done.2 = bf16[3,3,3,32,32]{4,3,2,1,0:T(8,128)(2,1)S(1)} copy-done((bf16[3,3,3,32,32]{4,3,2,1,0:T(8,128)(2,1)S(1)}, bf16[3,3,3,32,32]{4,3,2,1,0:T(8,128)(2,1)}, u32[]{:S(2)}) %copy-start.2) | copy-done | bytes 55320
  2.9 0.0 copy-start.3
  2.9 0.9 %copy-done.3 = bf16[3,3,3,32,32]{4,3,2,1,0:T(8,128)(2,1)S(1)} copy-done((bf16[3,3,3,32,32]{4,3,2,1,0:T(8,128)(2,1)S(1)}, bf16[3,3,3,32,32]{4,3,2,1,0:T(8,128)(2,1)}, u32[]{:S(2)}) %copy-start.3) | copy-done | bytes 55320
  3.9 0.0 copy-start.4
  3.9 0.9 %copy-done.4 = bf16[3,3,3,32,32]{4,3,2,1,0:T(8,128)(2,1)S(1)} copy-done((bf16[3,3,3,32,32]{4,3,2,1,0:T(8,128)(2,1)S(1)}, bf16[3,3,3,32,32]{4,3,2,1,0:T(8,128)(2,1)}, u32[]{:S(2)}) %copy-start.4) | copy-done | bytes 55320
  4.8 0.0 copy-start.5
  4.8 0.7 %copy-done.5 = bf16[32,32]{1,0:T(8,128)(2,1)S(1)} copy-done((bf16[32,32]{1,0:T(8,128)(2,1)S(1)}, bf16[32,32]{1,0:T(8,128)(2,1)}, u32[]{:S(2)}) %copy-start.5) | copy-done | bytes 2072
  5.5 28.9 %shard_map.64 = bf16[32,8,8,128]{3,2,1,0:T(8,128)(2,1)S(1)} custom-call(bf16[32,8,8,128]{3,2,1,0:T(8,128)(2,1)S(1)} %copy-done, bf16[32,32]{1,0:T(8,128)(2,1)S(1)} %copy-done.5, bf16[864,32]{1,0:T(8,128)(2,1)S(1)} %bitcast.4, bf16[864,32]{1,0:T(8,128)(2,1)S(1)} %bitcast.5, bf16[864,32]{1,0:T(8,128)(2,1)S(1)} %bitcast.6, bf16[864,32]{1,0:T(8,128)(2,1)S(1)} %bitcast.7), custom_call_target="tpu_custom_call" | custom-call | tf_op jit(solution)/shard_map/pallas_call | solution.py:422
  34.4 0.8 %copy.8 = bf16[32,8,8,128]{3,2,1,0:T(8,128)(2,1)} copy(bf16[32,8,8,128]{3,2,1,0:T(8,128)(2,1)S(1)} %shard_map.64) | data formatting | bytes 1048576
Async XLA Ops:
  0.0 1.0 %copy-start = (bf16[32,8,8,128]{3,2,1,0:T(8,128)(2,1)S(1)}, bf16[32,8,8,128]{3,2,1,0:T(8,128)(2,1)}, u32[]{:S(2)}) copy-start(bf16[32,8,8,128]{3,2,1,0:T(8,128)(2,1)} %field.1) | copy-start | bytes 1572868
  1.0 0.9 %copy-start.1 = (bf16[3,3,3,32,32]{4,3,2,1,0:T(8,128)(2,1)S(1)}, bf16[3,3,3,32,32]{4,3,2,1,0:T(8,128)(2,1)}, u32[]{:S(2)}) copy-start(bf16[3,3,3,32,32]{4,3,2,1,0:T(8,128)(2,1)} %param.8) | copy-start | bytes 165892
  2.0 0.9 %copy-start.2 = (bf16[3,3,3,32,32]{4,3,2,1,0:T(8,128)(2,1)S(1)}, bf16[3,3,3,32,32]{4,3,2,1,0:T(8,128)(2,1)}, u32[]{:S(2)}) copy-start(bf16[3,3,3,32,32]{4,3,2,1,0:T(8,128)(2,1)} %param.9) | copy-start | bytes 165892
  2.9 0.9 %copy-start.3 = (bf16[3,3,3,32,32]{4,3,2,1,0:T(8,128)(2,1)S(1)}, bf16[3,3,3,32,32]{4,3,2,1,0:T(8,128)(2,1)}, u32[]{:S(2)}) copy-start(bf16[3,3,3,32,32]{4,3,2,1,0:T(8,128)(2,1)} %param.10) | copy-start | bytes 165892
  3.9 0.9 %copy-start.4 = (bf16[3,3,3,32,32]{4,3,2,1,0:T(8,128)(2,1)S(1)}, bf16[3,3,3,32,32]{4,3,2,1,0:T(8,128)(2,1)}, u32[]{:S(2)}) copy-start(bf16[3,3,3,32,32]{4,3,2,1,0:T(8,128)(2,1)} %param.11) | copy-start | bytes 165892
  4.8 0.7 %copy-start.5 = (bf16[32,32]{1,0:T(8,128)(2,1)S(1)}, bf16[32,32]{1,0:T(8,128)(2,1)}, u32[]{:S(2)}) copy-start(bf16[32,32]{1,0:T(8,128)(2,1)} %mixing.1) | copy-start | bytes 6148

commit v3 on v2

--- a/solution.py
+++ b/solution.py
@@ -37,8 +37,8 @@
     return jnp.dot(a, b, preferred_element_type=F32)
 
 
-def kernel(counts, field, mixing, raw_fine, raw_half, raw_quarter, raw_eighth, out, u0, uc, u3x, u3y,
-           z0, zc, z3, v0, v1, v2, v3, zz1, zz2, zz3, qy0, y0, raw, wall, send, recv, loaded):
+def kernel(counts, field_in, mixing_in, raw_fine, raw_half, raw_quarter, raw_eighth, out, u0, uc, u2, u3x, u3y,
+           z0, zc, z2, z3, v0, v1, v2, v3, zz1, zz2, zz3, qy0, y0, raw, wall, field, mixing, send, recv, loaded):
     chans, bx, by, bz = field.shape
     cx, cy, cz = bx // 2, by // 2, bz // 2
     taps = raw_fine.shape[0]
@@ -66,10 +66,13 @@
         pltpu.make_async_copy(source, raw.at[k], loaded.at[k])
         for k, source in enumerate((raw_fine, raw_half, raw_quarter, raw_eighth))
     ]
+    loads.append(pltpu.make_async_copy(mixing_in, mixing, loaded.at[4]))
+    load_field = pltpu.make_async_copy(field_in, field, loaded.at[5])
+    load_field.start()
     for load in loads:
         load.start()
 
-    for ref in (uc, u3x, u3y):
+    for ref in (uc, u2, u3x, u3y):
         ref[...] = jnp.zeros_like(ref)
     for x in (0, bx + 1):
         u0[x] = jnp.zeros((by + 2, chans, bz), BF16)
@@ -78,7 +81,7 @@
     for side, d in ((0, -1), (1, 1)):
         @pl.when(jnp.logical_not(has((0, 0, d))))
         def _():
-            for ref in (z0, zc, z3):
+            for ref in (z0, zc, z2, z3):
                 ref[side] = jnp.zeros(ref.shape[1:], BF16)
 
     barrier = pltpu.get_barrier_semaphore()
@@ -93,6 +96,7 @@
     perm = jnp.where(perm_col == (perm_row % chans) * by + perm_row // chans, 1.0, 0.0).astype(BF16)
     back = jnp.where(perm_row == (perm_col % chans) * by + perm_col // chans, 1.0, 0.0).astype(BF16)
 
+    load_field.wait()
     for x in range(bx):
         slab = field[:, x].astype(F32).reshape(rows, bz).astype(BF16)
         u0[1 + x, 1 : 1 + by] = dot(perm, slab).astype(BF16).reshape(by, chans, bz)
@@ -112,11 +116,16 @@
 
     fine = [u0[1 + x, 1 + y].astype(F32) for x in range(bx) for y in range(by)]
     first = halve(quads(fine, bx, by), pair_sum(0, 0, bz))
-    second = halve(quads(first, cx, cy), pair_sum(0, cz, bz))
-    third = halve(quads(second, cx // 2, cy // 2), pair_sum(cz, 0, bz))
-    for x in range(cx):
+    second = halve(quads(first, cx, cy), pair_sum(0, 0, bz))
+    third = halve(quads(second, cx // 2, cy // 2), pair_sum(0, 0, bz))
+    for x in range(cx // 2):
         for y in range(cy):
-            uc[2 + x, 2 + y] = (first[x * cy + y] + second[(x % 2) * (cy // 2) + y % 2]).astype(BF16)
+            pair = first[2 * x * cy + y] + pltpu.roll(first[(2 * x + 1) * cy + y], cz, 1)
+            uc[1 + x, 2 + y] = pair.astype(BF16)
+    block = second[0]
+    for k in range(1, 4):
+        block = block + pltpu.roll(second[k], k * (cz // 2), 1)
+    u2[1, 1] = block.astype(BF16)
     u3x[2] = third[0].astype(BF16)
 
     peers = sum(has(d).astype(jnp.int32) for d in reach if possible(d))
@@ -157,15 +166,15 @@
             return depth, depth, length
         return (depth, length + depth, depth) if d < 0 else (length, 0, depth)
 
-    def rims(ref, length_x, length_y, depth):
+    around = [(dx, dy) for dx in (-1, 0, 1) for dy in (-1, 0, 1) if dx or dy]
+
+    def rims(ref, length_x, length_y, depth_x, depth_y):
         result = []
-        for dx in (-1, 0, 1):
-            for dy in (-1, 0, 1):
-                if dx or dy:
-                    sx, tx, wx = spans(dx, length_x, depth)
-                    sy, ty, wy = spans(dy, length_y, depth)
-                    result.append(copy((dx, dy, 0), ref.at[pl.ds(sx, wx), pl.ds(sy, wy)],
-                                       ref.at[pl.ds(tx, wx), pl.ds(ty, wy)]))
+        for dx, dy in around:
+            sx, tx, wx = spans(dx, length_x, depth_x)
+            sy, ty, wy = spans(dy, length_y, depth_y)
+            result.append(copy((dx, dy, 0), ref.at[pl.ds(sx, wx), pl.ds(sy, wy)],
+                               ref.at[pl.ds(tx, wx), pl.ds(ty, wy)]))
         return result
 
     def across(ref, dst, pieces):
@@ -174,23 +183,25 @@
             for d in (-1, 1) for piece in pieces
         ]
 
-    def frame(length_x, length_y, depth):
-        whole_y = pl.ds(0, length_y + 2 * depth)
-        mid_x = pl.ds(depth, length_x)
+    def frame(length_x, length_y, depth_x, depth_y):
+        whole_y = pl.ds(0, length_y + 2 * depth_y)
+        mid_x = pl.ds(depth_x, length_x)
         return [
-            (pl.ds(0, depth), whole_y), (pl.ds(length_x + depth, depth), whole_y),
-            (mid_x, pl.ds(0, depth)), (mid_x, pl.ds(length_y + depth, depth)),
+            (pl.ds(0, depth_x), whole_y), (pl.ds(length_x + depth_x, depth_x), whole_y),
+            (mid_x, pl.ds(0, depth_y)), (mid_x, pl.ds(length_y + depth_y, depth_y)),
         ]
 
     x_last = [copy((d, 0, 0), u3x.at[2], u3x.at[2 - d]) for d in (-1, 1, -2, 2)]
     y_last = [copy((0, d, 0), u3y.at[2], u3y.at[2 - d]) for d in (-1, 1, -2, 2)]
     z_last = [copy((0, 0, d), u3y, z3.at[(1 - d) // 2]) for d in (-1, 1)]
-    small = rims(uc, cx, cy, 2)
-    fine_rims = rims(u0, bx, by, 1)
-    z_own = across(uc, zc, [(pl.ds(2, cx), pl.ds(2, cy))])
+    small = rims(uc, cx // 2, cy, 1, 2)
+    small += [copy((dx, dy, 0), u2.at[1, 1], u2.at[1 - dx, 1 - dy]) for dx, dy in around]
+    fine_rims = rims(u0, bx, by, 1, 1)
+    z_own = across(uc, zc, [(pl.ds(1, cx // 2), pl.ds(2, cy))])
     z_own_fine = across(u0, z0, [(pl.ds(1, bx), pl.ds(1, by))])
-    z_small = across(uc, zc, frame(cx, cy, 2))
-    z_fine = across(u0, z0, frame(bx, by, 1))
+    z_small = across(uc, zc, frame(cx // 2, cy, 1, 2))
+    z_small += [copy((0, 0, d), u2, z2.at[(1 - d) // 2]) for d in (-1, 1)]
+    z_fine = across(u0, z0, frame(bx, by, 1, 1))
 
     start(x_last)
     start(small)
@@ -259,13 +270,6 @@
 
     lax.fori_loop(0, bx, fill_own, 0)
 
-    arrive(small)
-    start(z_small)
-    arrive(y_last)
-    start(z_last)
-    arrive(fine_rims)
-    start(z_fine)
-
     def interior(p, carry):
         for y in range(1, by - 1):
             fine_pair(1 + 2 * p, 2 + 2 * p, y)
@@ -273,29 +277,16 @@
 
     lax.fori_loop(0, (bx - 2) // 2, interior, 0)
 
+    arrive(y_last)
+    start(z_last)
+    arrive(small)
+    start(z_small)
     arrive(z_own)
-    arrive(z_small)
     arrive(z_last)
 
     for k in range(5):
         for y in range(5):
             v3[k, y] = window(u3y[y], z3[0, y], z3[1, y], k * width, width)
-
-    def fill2(x, carry):
-        source_x = jnp.where(x >= 4, x + 2, x)
-        for y in range(6):
-            sy = y + 2 if y >= 4 else y
-            v2[x, y] = window(uc[source_x, sy], zc[0, source_x, sy], zc[1, source_x, sy], cz, cz // 2)
-        return carry
-
-    lax.fori_loop(0, 6, fill2, 0)
-
-    def fill1(x, carry):
-        for y in range(cy + 4):
-            v1[x, y] = window(uc[x, y], zc[0, x, y], zc[1, x, y], 0, cz)
-        return carry
-
-    lax.fori_loop(0, cx + 4, fill1, 0)
 
     def rim(length):
         low = jnp.where(gz > 0, 1.0, 0.0)
@@ -344,9 +335,33 @@
                 zz[2 * i + 1, y] = ((value[:, bz:] + 0.75 * b + 0.25 * a)
                                     * (scale * inside(2 * i + 1, size_x, "gx"))).astype(BF16)
 
+    arrive(z_small)
+
+    def fill2(x, carry):
+        for k in range(2):
+            for y in range(6):
+                offset = (2 * k + y % 2) * (cz // 2)
+                v2[2 * x + k, y] = window(
+                    u2[x, y // 2], z2[0, x, y // 2], z2[1, x, y // 2], offset, cz // 2)
+        return carry
+
+    lax.fori_loop(0, 3, fill2, 0)
+
+    def fill1(x, carry):
+        for y in range(cy + 4):
+            own, low, high = uc[x, y], zc[0, x, y], zc[1, x, y]
+            for k in range(2):
+                v1[2 * x + k, y] = window(own, low, high, k * cz, cz)
+        return carry
+
+    lax.fori_loop(0, cx // 2 + 2, fill1, 0)
+
     q3 = raised(zz3, width, 1)
     qy3 = [along_y([q3[x, y] for y in range(3)], 4, 1) for x in range(3)]
     level(wall[2, :, pl.ds(0, taps)], v2, zz2, zz3, cx // 2, cy // 2, cz // 2, qy3)
+    arrive(fine_rims)
+    start(z_fine)
+
     q2 = raised(zz2, cz // 2, 1)
     qy2 = [along_y([q2[x, y] for y in range(cy // 2 + 2)], cy + 2, 1) for x in range(cx // 2 + 2)]
     level(wall[1, :, pl.ds(0, taps)], v1, zz1, zz2, cx, cy, cz, qy2)
@@ -412,32 +427,33 @@
         rows = [k.reshape(-1, chans) for k in kernels]
         taps = rows[0].shape[0]
         vmem = pl.BlockSpec(memory_space=pltpu.VMEM)
-        anywhere = pl.BlockSpec(memory_space=pl.ANY)
+        remote = pl.BlockSpec(memory_space=pltpu.HBM)
 
         def buf(*dims, dtype=BF16):
             return pltpu.VMEM(dims, dtype)
 
         fine = (bx + 2, by + 2, chans, bz)
-        coarse = (cx + 4, cy + 4, chans, bz)
+        coarse = (cx // 2 + 2, cy + 4, chans, bz)
         return pl.pallas_call(
             functools.partial(kernel, counts),
             out_shape=jax.ShapeDtypeStruct(field.shape, BF16),
-            in_specs=[vmem] * 2 + [anywhere] * 4,
+            in_specs=[remote] * 6,
             out_specs=vmem,
             scratch_shapes=[
-                buf(*fine), buf(*coarse), buf(5, chans, bz), buf(5, chans, bz),
-                buf(2, *fine), buf(2, *coarse), buf(2, 5, chans, bz),
+                buf(*fine), buf(*coarse), buf(3, 3, chans, bz), buf(5, chans, bz), buf(5, chans, bz),
+                buf(2, *fine), buf(2, *coarse), buf(2, 3, 3, chans, bz), buf(2, 5, chans, bz),
                 buf(bx + 2, by + 2, 3 * chans, bz),
                 buf(cx + 4, cy + 4, 3 * chans, bz),
                 buf(6, 6, 3 * chans, bz), buf(5, 5, 3 * chans, bz),
                 buf(cx + 2, cy + 2, chans, bz), buf(4, 4, chans, bz), buf(3, 3, chans, bz),
                 buf(cx + 2, by, chans, bz, dtype=F32), buf(bx, by, chans, bz, dtype=F32),
                 buf(4, taps, chans), buf(4, chans, taps + chans),
-                pltpu.SemaphoreType.DMA((48,)), pltpu.SemaphoreType.DMA((48,)),
-                pltpu.SemaphoreType.DMA((4,)),
+                buf(*field.shape), buf(*mixing.shape),
+                pltpu.SemaphoreType.DMA((64,)), pltpu.SemaphoreType.DMA((64,)),
+                pltpu.SemaphoreType.DMA((6,)),
             ],
             compiler_params=pltpu.CompilerParams(
-                collective_id=0, has_side_effects=True, vmem_limit_bytes=24 * 2**20),
+                collective_id=0, has_side_effects=True, vmem_limit_bytes=56 * 2**20),
         )(field, mixing, *rows)
 
     placed = (P(None, "gx", "gy", "gz"), P(), P(), P(), P(), P())

time: 35.5 us -> 29.5 us (0.83)
  the two profiles are of different devices: /device:TPU:12 before, /device:TPU:13 now
where the time goes in v3:
time: 29.5 us; the launch traced here: 29.3 us
  Pallas kernels  27.4 us (93%)
  local copies, waits for them, and re-layouts  1.87 us (6%)
    pallas_call x1, Pallas kernels, on_device(): pl.pallas_call(functools.partial(kernel, counts), out_shape=jax.ShapeDtyp...  27.4 us
    unnamed x1, local copies, waits for them, and re-layouts  1.87 us

profile of v3, /device:TPU:13, one launch (start us, length us, event | category | flops | bytes accessed | tf_op | source)
XLA Modules:
  0.0 29.3 jit_solution(224197791838088740)
XLA Ops:
  0.0 27.4 %shard_map.64 = bf16[32,8,8,128]{3,2,1,0:T(8,128)(2,1)} custom-call(bf16[32,8,8,128]{3,2,1,0:T(8,128)(2,1)} %field_in.1, bf16[32,32]{1,0:T(8,128)(2,1)} %mixing_in.1, bf16[864,32]{1,0:T(8,128)(2,1)} %bitcast.4, bf16[864,32]{1,0:T(8,128)(2,1)} %bitcast.5, bf16[864,32]{1,0:T(8,128)(2,1)} %bitcast.6, bf16[864,32]{1,0:T(8,128)(2,1)} %bitcast.7), custom_call_target="tpu_custom_call" | custom-call | tf_op jit(solution)/shard_map/pallas_call | solution.py:437
  27.4 1.9 %copy.8 = bf16[32,8,8,128]{3,2,1,0:T(8,128)(2,1)} copy(bf16[32,8,8,128]{3,2,1,0:T(8,128)(2,1)} %shard_map.64) | data formatting | bytes 1048576

commit v4 on v3

--- a/solution.py
+++ b/solution.py
@@ -236,18 +236,20 @@
         return value if amount == 0 else pltpu.roll(value, amount, 1)
 
     def window(own, low, high, offset, length):
-        own, low, high = own.astype(F32), low.astype(F32), high.astype(F32)
-        value = jnp.where(lane < 2, roll(low, 2 - offset - length), 0.0)
-        value = jnp.where((lane >= 2) & (lane < length + 2), roll(own, 2 - offset), value)
-        value = jnp.where((lane >= length + 2) & (lane < length + 4), roll(high, length + 2 - offset), value)
-        return jnp.concatenate([roll(value, -dz) for dz in range(3)], axis=0).astype(BF16)
+        edge = (lane < 2) | ((lane >= length + 2) & (lane < length + 4))
+        if 2 * length % bz == 0:
+            outer = roll(jnp.where(lane >= offset + 2, low, high), 2 - offset - length)
+        else:
+            outer = jnp.where(lane < 2, roll(low, 2 - offset - length), roll(high, length + 2 - offset))
+        zero = jnp.zeros_like(own)
+        value = jnp.where(lane < length + 4, jnp.where(edge, outer, roll(own, 2 - offset)), zero)
+        return jnp.concatenate([roll(value, -dz) for dz in range(3)], axis=0)
 
     def fill_fine(x, y):
         own = u0[x, y]
-        wide = own.astype(F32)
-        low = jnp.where(lane == bz - 1, z0[0, x, y].astype(F32), wide)
-        high = jnp.where(lane == 0, z0[1, x, y].astype(F32), wide)
-        v0[x, y] = jnp.concatenate([roll(low, 1).astype(BF16), own, roll(high, -1).astype(BF16)], axis=0)
+        low = jnp.where(lane == bz - 1, z0[0, x, y], own)
+        high = jnp.where(lane == 0, z0[1, x, y], own)
+        v0[x, y] = jnp.concatenate([roll(low, 1), own, roll(high, -1)], axis=0)
 
     def patches(v, x, y):
         return jnp.concatenate(

time: 29.5 us -> 27 us (0.915)
  Pallas kernels: 27.4 us -> 25 us
    pallas_call x1, Pallas kernels: 27.4 us -> 25 us  [on_device(): pl.pallas_call(functools.partial(kernel, counts), out_shape=jax.ShapeDtyp...]
where the time goes in v4:
time: 27 us; the launch traced here: 26.8 us
  Pallas kernels  25 us (93%)
  local copies, waits for them, and re-layouts  1.87 us (7%)
    pallas_call x1, Pallas kernels, on_device(): pl.pallas_call(functools.partial(kernel, counts), out_shape=jax.ShapeDtyp...  25 us
    unnamed x1, local copies, waits for them, and re-layouts  1.87 us

profile of v4, /device:TPU:13, one launch (start us, length us, event | category | flops | bytes accessed | tf_op | source)
XLA Modules:
  0.0 26.8 jit_solution(17513349256471510663)
XLA Ops:
  0.0 25.0 %shard_map.64 = bf16[32,8,8,128]{3,2,1,0:T(8,128)(2,1)} custom-call(bf16[32,8,8,128]{3,2,1,0:T(8,128)(2,1)} %field_in.1, bf16[32,32]{1,0:T(8,128)(2,1)} %mixing_in.1, bf16[864,32]{1,0:T(8,128)(2,1)} %bitcast.4, bf16[864,32]{1,0:T(8,128)(2,1)} %bitcast.5, bf16[864,32]{1,0:T(8,128)(2,1)} %bitcast.6, bf16[864,32]{1,0:T(8,128)(2,1)} %bitcast.7), custom_call_target="tpu_custom_call" | custom-call | tf_op jit(solution)/shard_map/pallas_call | solution.py:439
  25.0 1.9 %copy.8 = bf16[32,8,8,128]{3,2,1,0:T(8,128)(2,1)} copy(bf16[32,8,8,128]{3,2,1,0:T(8,128)(2,1)} %shard_map.64) | data formatting | bytes 1048576
